TPU v7x, 32 devices: a whole 2x2x4 slice. The times are simulated.
32 devices in a mesh: stream: 16 (over z, y, core), tm: 2 (over x).
Axes of the slice: x: 2, y: 2, z: 4, core: 2. Of those that a mesh axis runs over, the one named last changes fastest.
Arguments:
- signal: bfloat16 [32, 2, 1048576], P('stream', None, 'tm'), parts along dimension 0, may hold values from -11 to 11
- taps: float32 [16, 4096], replicated, may hold values from -1.5 to 1.5
Outputs:
- channels_out: float32 [32, 2, 4096, 256], P('stream', None, 'tm'), parts along dimension 0
There are 16 independent parts, one for each index of `stream`. A program takes and returns all parts, laid end to end along the dimension named above; an argument that names none is the same for every part. Nothing has to cross between parts.
All inputs are finite; a program needn't handle non-finite values.
Results may differ from a plain program's by a relative error of at most 0.0003.
Values may be sent and summed in bfloat16 or wider, within the bound.
A program may use at most 128 MiB of HBM per device.

v0:
```python
import functools
import math

import jax
import jax.numpy as jnp
import numpy as np
from jax import lax
from jax.experimental import pallas as pl
from jax.experimental.pallas import tpu as pltpu
from jax.sharding import PartitionSpec as P

LANES = 128
GROUP = 4
PAIR = 2 * GROUP


def angles(height, breadth, modulus):
    product = np.arange(height)[:, None] * np.arange(breadth)[None, :] % modulus
    return product * (2.0 * math.pi / modulus)


def split(table):
    high = table.astype(np.float32).astype(jnp.bfloat16)
    low = (table - high.astype(np.float64)).astype(np.float32).astype(jnp.bfloat16)
    return high, low


def first_table(rows):
    turn = angles(rows, rows, rows)
    cos, sin = np.cos(turn), np.sin(turn)
    whole = np.block([[cos, sin], [-sin, cos]])
    high, low = split(np.kron(np.eye(GROUP), whole))
    return np.concatenate([high, low, high], axis=1)


def second_table(rows, channels, parts):
    turn = angles(LANES, LANES, LANES)
    scale = 1.0 / math.isqrt(channels)
    cos, sin = np.cos(turn) * scale, np.sin(turn) * scale
    each = LANES // parts
    blocks = []
    for part in range(parts):
        pick = slice(part * each, (part + 1) * each)
        blocks.append(np.block([[cos[pick], sin[pick]], [-sin[pick], cos[pick]]]))
    high, low = split(np.concatenate(blocks, axis=0))
    return np.concatenate([high, low, high], axis=1)


def transform_kernel(parts, frames, rows, edge, x_ref, halo_ref, taps_ref, first_ref, cos_ref,
                     sin_ref, second_ref, own_ref, away_ref, wide, grid, zr, zi):
    depth = edge
    for p in range(2):
        wide[p, :edge] = halo_ref[0, p].astype(jnp.float32)

    @pl.loop(0, frames // PAIR)
    def _(step):
        base = pl.multiple_of(step * PAIR, PAIR)
        for p in range(2):
            wide[p, pl.ds(base + edge, PAIR)] = x_ref[0, p, pl.ds(base, PAIR)].astype(jnp.float32)

    @pl.loop(0, frames // PAIR)
    def _(step):
        base = pl.multiple_of(step * PAIR, PAIR)
        for p in range(2):
            for piece in range(rows // 8):
                sub = slice(piece * 8, piece * 8 + 8)
                data = [wide[p, base + 1 + i, sub, :] for i in range(PAIR + depth - 1)]
                taps = [taps_ref[k, sub, :] for k in range(depth)]
                for t in range(PAIR):
                    total = taps[0] * data[t + depth - 1]
                    for k in range(1, depth):
                        total = total + taps[k] * data[t + depth - 1 - k]
                    row = ((t % GROUP) * 2 + p) * rows + piece * 8
                    lane = (t // GROUP) * LANES
                    grid[row : row + 8, lane : lane + LANES] = total
        value = grid[...]
        high = value.astype(jnp.bfloat16)
        low = (value - high.astype(jnp.float32)).astype(jnp.bfloat16)
        out = jnp.dot(first_ref[...], jnp.concatenate([high, high, low], axis=0),
                      preferred_element_type=jnp.float32)
        cos, sin = cos_ref[...], sin_ref[...]
        for t in range(PAIR):
            row = (t % GROUP) * 2 * rows
            lane = (t // GROUP) * LANES
            real = out[row : row + rows, lane : lane + LANES]
            imag = out[row + rows : row + 2 * rows, lane : lane + LANES]
            at = pl.multiple_of((base + t) * rows, rows)
            zr[pl.ds(at, rows), :] = real * cos + imag * sin
            zi[pl.ds(at, rows), :] = imag * cos - real * sin

    each = LANES // parts

    @pl.loop(0, rows // 2)
    def _(step):
        pieces = []
        for i in range(2):
            pick = pl.ds(step * 2 + i, frames, stride=rows)
            pieces.append(jnp.concatenate([zr[pick, :], zi[pick, :]], axis=1))
        value = jnp.concatenate(pieces, axis=0)
        high = value.astype(jnp.bfloat16)
        low = (value - high.astype(jnp.float32)).astype(jnp.bfloat16)
        out = lax.dot_general(second_ref[...], jnp.concatenate([high, high, low], axis=1),
                              (((1,), (1,)), ((), ())), preferred_element_type=jnp.float32)
        for i in range(2):
            c = step * 2 + i
            lane = slice(i * frames, (i + 1) * frames)
            for p in range(2):
                own_ref[p, c] = out[p * each : (p + 1) * each, lane]
                for k in range(1, parts):
                    top = (2 * k + p) * each
                    away_ref[k - 1, p, c] = out[top : top + each, lane]


def finish_kernel(parts, frames, rows, each, *refs):
    own_ref, away_refs, out_ref, turned = refs[0], refs[1:parts], refs[-2], refs[-1]
    me = lax.axis_index("tm")

    @pl.loop(0, rows, unroll=8)
    def _(c):
        data = [[own_ref[p, c] for p in range(2)]]
        for ref in away_refs:
            data.append([ref[p, c] for p in range(2)])
        square = sum(d[0] * d[0] + d[1] * d[1] for d in data)
        power = jnp.sum(square, axis=1, keepdims=True)
        factor = lax.rsqrt(power * (1.0 / (frames * parts)) + 1.0)
        for k in range(parts):
            for p in range(2):
                turned[k, p, pl.ds(c, each, stride=rows), :] = data[k][p] * factor

    for k in range(parts):
        source = lax.rem(me + parts - k, parts)
        lane = pl.ds(pl.multiple_of(source * frames, frames), frames)
        for p in range(2):
            out_ref[0, p, :, lane] = turned[k, p]


def sent(block, route):
    narrow = (block * 2.0).astype(jnp.float16)
    return lax.ppermute(narrow, "tm", route).astype(jnp.float32) * 0.5


def shards(parts, signal, taps):
    streams = signal.shape[0]
    depth, channels = taps.shape
    rows = channels // LANES
    frames = signal.shape[2] // channels
    each = LANES // parts
    me = lax.axis_index("tm")
    x = signal.reshape(streams, 2, frames, rows, LANES)
    route = [(i, i + 1) for i in range(parts - 1)]
    halos = [lax.ppermute(x[s : s + 1, :, frames - depth :], "tm", route) for s in range(streams)]
    taps = taps.reshape(depth, rows, LANES)
    twist = angles(rows, LANES, channels)
    cos, sin = jnp.asarray(np.cos(twist), jnp.float32), jnp.asarray(np.sin(twist), jnp.float32)
    first = jnp.asarray(first_table(rows))
    table = second_table(rows, channels, parts)
    second = lax.dynamic_slice(
        jnp.asarray(np.concatenate([table, table], axis=0)),
        (me * 2 * each, 0), table.shape)
    owns, aways = [], []
    whole = lambda a: pl.BlockSpec(a.shape, lambda i, nd=a.ndim: (0,) * nd)
    for s in range(streams):
        pick = lambda i, s=s: (s, 0, 0, 0, 0)
        own, away = pl.pallas_call(
            functools.partial(transform_kernel, parts, frames, rows, depth),
            grid=(1,),
            in_specs=[
                pl.BlockSpec((1, 2, frames, rows, LANES), pick),
                whole(halos[s]), whole(taps), whole(first), whole(cos), whole(sin), whole(second),
            ],
            out_specs=[
                pl.BlockSpec((2, rows, each, frames), lambda i: (0, 0, 0, 0)),
                pl.BlockSpec((parts - 1, 2, rows, each, frames), lambda i: (0, 0, 0, 0, 0)),
            ],
            out_shape=[
                jax.ShapeDtypeStruct((2, rows, each, frames), jnp.float32),
                jax.ShapeDtypeStruct((parts - 1, 2, rows, each, frames), jnp.float32),
            ],
            scratch_shapes=[
                pltpu.VMEM((2, depth + frames, rows, LANES), jnp.float32),
                pltpu.VMEM((2 * GROUP * rows, 2 * LANES), jnp.float32),
                pltpu.VMEM((frames * rows, LANES), jnp.float32),
                pltpu.VMEM((frames * rows, LANES), jnp.float32),
            ],
            compiler_params=pltpu.CompilerParams(vmem_limit_bytes=48 << 20),
            cost_estimate=pl.CostEstimate(flops=8 * 10**9, bytes_accessed=8 << 20, transcendentals=0),
            name="transform",
        )(x, halos[s], taps, first, cos, sin, second)
        owns.append(own)
        aways.append([
            sent(away[k - 1], [(i, (i + k) % parts) for i in range(parts)])
            for k in range(1, parts)
        ])
    result = None
    step = 16
    shape = jax.ShapeDtypeStruct((streams, 2, channels // parts, frames * parts), jnp.float32)
    for s in range(streams):
        block = pl.BlockSpec((2, rows, step, frames), lambda i: (0, 0, i, 0))
        args = [owns[s], *aways[s]]
        specs = [block] * parts
        alias = {}
        if result is not None:
            alias = {len(args): 0}
            args.append(result)
            specs.append(pl.BlockSpec(memory_space=pl.ANY))
        result = pl.pallas_call(
            functools.partial(finish_kernel, parts, frames, rows, step),
            grid=(each // step,),
            in_specs=specs,
            out_specs=pl.BlockSpec((1, 2, rows * step, frames * parts), lambda i, s=s: (s, 0, i, 0)),
            out_shape=shape,
            input_output_aliases=alias,
            scratch_shapes=[pltpu.VMEM((parts, 2, rows * step, frames), jnp.float32)],
            compiler_params=pltpu.CompilerParams(vmem_limit_bytes=48 << 20),
            cost_estimate=pl.CostEstimate(flops=10**8, bytes_accessed=8 << 20, transcendentals=0),
            name="finish",
        )(*args)
    return result


def solution(mesh):
    in_specs = (P("stream", None, "tm"), P())
    out_specs = P("stream", None, "tm", None)
    body = functools.partial(shards, mesh.shape["tm"])
    return jax.shard_map(body, mesh=mesh, in_specs=in_specs, out_specs=out_specs, check_vma=False)
```

profile of v0, /device:TPU:0, one launch (start us, length us, event | category | flops | bytes accessed | tf_op | source)
XLA Modules:
  0.0 91.7 jit_solution(11891468349066390697)
XLA Ops:
  0.0 0.0 copy-start.4
  0.0 0.0 copy-start.3
  0.0 6.1 %reshape.12.x_ref = bf16[2,2,128,32,128]{4,3,2,1,0:T(8,128)(2,1)} reshape(bf16[2,2,524288]{2,1,0:T(2,128)(2,1)} %param.6) | data formatting | bytes 8388608 | tf_op jit(solution)/shard_map/reshape | solution.py:149
  6.1 0.0 copy-start
  6.1 0.0 copy-start.1
  6.1 0.0 copy-start.2
  6.1 1.1 %fusion.2 = (bf16[1,2,16,32,128]{4,3,2,1,0:T(8,128)(2,1)S(1)}, bf16[1,2,16,32,128]{4,3,2,1,0:T(8,128)(2,1)S(1)}) fusion(bf16[2,2,128,32,128]{4,3,2,1,0:T(8,128)(2,1)} %reshape.12.x_ref), kind=kLoop, calls=%fused_computation.7 | loop fusion | bytes 1048576 | tf_op jit(solution)/shard_map/slice | solution.py:151
  7.2 4.9 %collective-permute-start.2 = (bf16[1,2,16,32,128]{4,3,2,1,0:T(8,128)(2,1)S(1)}, bf16[1,2,16,32,128]{4,3,2,1,0:T(8,128)(2,1)S(1)}, u32[]{:S(2)}, u32[]{:S(2)}) collective-permute-start(bf16[1,2,16,32,128]{4,3,2,1,0:T(8,128)(2,1)S(1)} %get-tuple-element.13), channel_id=1, source_target_pairs={{0,1},{2,3},{4,5},{6,7},{8,9},{10,11},{12,13},{14,15},{16,17},{18,... | collective-permute-start | bytes 786440 | tf_op jit(solution)/shard_map/ppermute | solution.py:151
  12.1 1.3 %collective-permute-start = (bf16[1,2,16,32,128]{4,3,2,1,0:T(8,128)(2,1)S(1)}, bf16[1,2,16,32,128]{4,3,2,1,0:T(8,128)(2,1)S(1)}, u32[]{:S(2)}, u32[]{:S(2)}) collective-permute-start(bf16[1,2,16,32,128]{4,3,2,1,0:T(8,128)(2,1)S(1)} %get-tuple-element.14), channel_id=1, source_target_pairs={{0,1},{2,3},{4,5},{6,7},{8,9},{10,11},{12,13},{14,15},{16,17},{18,... | collective-permute-start | bytes 786440 | tf_op jit(solution)/shard_map/ppermute | solution.py:151
  13.5 0.0 copy-done.3
  13.5 0.1 copy.8
  13.5 0.0 copy-done.4
  13.6 5.2 %collective-permute-done.2.halo_ref = bf16[1,2,16,32,128]{4,3,2,1,0:T(8,128)(2,1)S(1)} collective-permute-done((bf16[1,2,16,32,128]{4,3,2,1,0:T(8,128)(2,1)S(1)}, bf16[1,2,16,32,128]{4,3,2,1,0:T(8,128)(2,1)S(1)}, u32[]{:S(2)}, u32[]{:S(2)}) %collective-permute-start.2) | collective-permute-done | bytes 262176 | tf_op jit(solution)/shard_map/ppermute | solution.py:151
  18.8 0.0 copy-done
  18.8 0.0 copy-done.1
  18.8 0.0 copy-done.2
  18.8 19.0 %transform.3 = (f32[2,32,64,128]{3,2,1,0:T(8,128)S(1)}, f32[1,2,32,64,128]{4,3,2,1,0:T(8,128)S(1)}) custom-call(bf16[2,2,128,32,128]{4,3,2,1,0:T(8,128)(2,1)} %reshape.12.x_ref, bf16[1,2,16,32,128]{4,3,2,1,0:T(8,128)(2,1)S(1)} %collective-permute-done.2.halo_ref, f32[16,32,128]{2,1,0:T(8,128)S(1)} %bitcast.6, bf16[256,768]{1,0:T(8,128)(2,1)S(1)} %copy-done, ...), custom_call_target="tpu_custom_call" | custom-call | flops 8000000000 | bytes 8388608 | tf_op jit(solution)/shard_map/transform/pallas_call | solution.py:164
  37.8 0.3 fusion.1
  38.1 2.5 %collective-permute-start.3 = (f16[2,32,64,128]{3,2,1,0:T(8,128)(2,1)S(1)}, f16[2,32,64,128]{3,2,1,0:T(8,128)(2,1)S(1)}, u32[]{:S(2)}, u32[]{:S(2)}) collective-permute-start(f16[2,32,64,128]{3,2,1,0:T(8,128)(2,1)S(1)} %fusion.1), channel_id=1, source_target_pairs={{0,1},{1,0},{2,3},{3,2},{4,5},{5,4},{6,7},{7,6},{8,9},{9,8},{10,11... | collective-permute-start | bytes 3145736 | tf_op jit(solution)/shard_map/ppermute | solution.py:139
  40.6 0.0 collective-permute-done.halo_ref
  40.6 19.0 %transform.2 = (f32[2,32,64,128]{3,2,1,0:T(8,128)S(1)}, f32[1,2,32,64,128]{4,3,2,1,0:T(8,128)S(1)}) custom-call(bf16[2,2,128,32,128]{4,3,2,1,0:T(8,128)(2,1)} %reshape.12.x_ref, bf16[1,2,16,32,128]{4,3,2,1,0:T(8,128)(2,1)S(1)} %collective-permute-done.halo_ref, f32[16,32,128]{2,1,0:T(8,128)S(1)} %bitcast.7, bf16[256,768]{1,0:T(8,128)(2,1)S(1)} %copy-done, ...), custom_call_target="tpu_custom_call" | custom-call | flops 8000000000 | bytes 8388608 | tf_op jit(solution)/shard_map/transform/pallas_call | solution.py:164
  59.7 0.3 fusion
  60.0 0.1 collective-permute-start.1
  60.0 4.1 %collective-permute-done.3 = f16[2,32,64,128]{3,2,1,0:T(8,128)(2,1)S(1)} collective-permute-done((f16[2,32,64,128]{3,2,1,0:T(8,128)(2,1)S(1)}, f16[2,32,64,128]{3,2,1,0:T(8,128)(2,1)S(1)}, u32[]{:S(2)}, u32[]{:S(2)}) %collective-permute-start.3) | collective-permute-done | bytes 1048608 | tf_op jit(solution)/shard_map/ppermute | solution.py:139
  64.1 0.3 convert_multiply_fusion.refs_1_
  64.4 7.2 %finish.2.refs_2_ = f32[2,2,2048,256]{3,2,1,0:T(8,128)} custom-call(f32[2,32,64,128]{3,2,1,0:T(8,128)S(1)} %get-tuple-element.11.refs_0_, f32[2,32,64,128]{3,2,1,0:T(8,128)S(1)} %convert_multiply_fusion.refs_1_), custom_call_target="tpu_custom_call" | custom-call | flops 100000000 | bytes 8388608 | tf_op jit(solution)/shard_map/finish/pallas_call | solution.py:206
  71.6 12.7 %collective-permute-done.1 = f16[2,32,64,128]{3,2,1,0:T(8,128)(2,1)S(1)} collective-permute-done((f16[2,32,64,128]{3,2,1,0:T(8,128)(2,1)S(1)}, f16[2,32,64,128]{3,2,1,0:T(8,128)(2,1)S(1)}, u32[]{:S(2)}, u32[]{:S(2)}) %collective-permute-start.1) | collective-permute-done | bytes 1048608 | tf_op jit(solution)/shard_map/ppermute | solution.py:139
  84.3 0.3 convert_multiply_fusion.1.refs_1_
  84.5 7.2 %finish.3 = f32[2,2,2048,256]{3,2,1,0:T(8,128)} custom-call(f32[2,32,64,128]{3,2,1,0:T(8,128)S(1)} %get-tuple-element.9.refs_0_, f32[2,32,64,128]{3,2,1,0:T(8,128)S(1)} %convert_multiply_fusion.1.refs_1_, f32[2,2,2048,256]{3,2,1,0:T(8,128)} %finish.2.refs_2_), custom_call_target="tpu_custom_call", output_to_operand_aliasing={{}: (2, {})} | custom-call | flops 100000000 | bytes 8388608 | tf_op jit(solution)/shard_map/finish/pallas_call | solution.py:206
  (1 shorter events, 0.0 us)
Async XLA Ops:
  0.0 13.5 %copy-start.4 = (bf16[512,768]{1,0:T(8,128)(2,1)S(1)}, bf16[512,768]{1,0:T(8,128)(2,1)}, u32[]{:S(2)}) copy-start(bf16[512,768]{1,0:T(8,128)(2,1)} %constant.27.clone) | copy-start | bytes 2359300
  0.0 13.5 %copy-start.3 = (f32[16,4096]{1,0:T(8,128)S(1)}, f32[16,4096]{1,0:T(8,128)}, u32[]{:S(2)}) copy-start(f32[16,4096]{1,0:T(8,128)} %param.7) | copy-start | bytes 786436
  6.1 12.7 %copy-start = (bf16[256,768]{1,0:T(8,128)(2,1)S(1)}, bf16[256,768]{1,0:T(8,128)(2,1)}, u32[]{:S(2)}) copy-start(bf16[256,768]{1,0:T(8,128)(2,1)} %constant.26.clone.first_ref) | copy-start | bytes 1179652
  6.1 12.7 %copy-start.1 = (f32[32,128]{1,0:T(8,128)S(1)}, f32[32,128]{1,0:T(8,128)}, u32[]{:S(2)}) copy-start(f32[32,128]{1,0:T(8,128)} %constant.25.clone.sin_ref) | copy-start | bytes 49156
  6.1 12.7 %copy-start.2 = (f32[32,128]{1,0:T(8,128)S(1)}, f32[32,128]{1,0:T(8,128)}, u32[]{:S(2)}) copy-start(f32[32,128]{1,0:T(8,128)} %constant.24.clone.cos_ref) | copy-start | bytes 49156
  7.2 11.6 %collective-permute-start.2 = (bf16[1,2,16,32,128]{4,3,2,1,0:T(8,128)(2,1)S(1)}, bf16[1,2,16,32,128]{4,3,2,1,0:T(8,128)(2,1)S(1)}, u32[]{:S(2)}, u32[]{:S(2)}) collective-permute-start(bf16[1,2,16,32,128]{4,3,2,1,0:T(8,128)(2,1)S(1)} %get-tuple-element.13), channel_id=1, source_target_pairs={{0,1},{2,3},{4,5},{6,7},{8,9},{10,11},{12,13},{14,15},{16,17},{18,... | collective-permute-start | bytes 786440 | tf_op jit(solution)/shard_map/ppermute | solution.py:151
  12.1 28.5 %collective-permute-start = (bf16[1,2,16,32,128]{4,3,2,1,0:T(8,128)(2,1)S(1)}, bf16[1,2,16,32,128]{4,3,2,1,0:T(8,128)(2,1)S(1)}, u32[]{:S(2)}, u32[]{:S(2)}) collective-permute-start(bf16[1,2,16,32,128]{4,3,2,1,0:T(8,128)(2,1)S(1)} %get-tuple-element.14), channel_id=1, source_target_pairs={{0,1},{2,3},{4,5},{6,7},{8,9},{10,11},{12,13},{14,15},{16,17},{18,... | collective-permute-start | bytes 786440 | tf_op jit(solution)/shard_map/ppermute | solution.py:151
  38.1 26.0 %collective-permute-start.3 = (f16[2,32,64,128]{3,2,1,0:T(8,128)(2,1)S(1)}, f16[2,32,64,128]{3,2,1,0:T(8,128)(2,1)S(1)}, u32[]{:S(2)}, u32[]{:S(2)}) collective-permute-start(f16[2,32,64,128]{3,2,1,0:T(8,128)(2,1)S(1)} %fusion.1), channel_id=1, source_target_pairs={{0,1},{1,0},{2,3},{3,2},{4,5},{5,4},{6,7},{7,6},{8,9},{9,8},{10,11... | collective-permute-start | bytes 3145736 | tf_op jit(solution)/shard_map/ppermute | solution.py:139
  60.0 24.3 %collective-permute-start.1 = (f16[2,32,64,128]{3,2,1,0:T(8,128)(2,1)S(1)}, f16[2,32,64,128]{3,2,1,0:T(8,128)(2,1)S(1)}, u32[]{:S(2)}, u32[]{:S(2)}) collective-permute-start(f16[2,32,64,128]{3,2,1,0:T(8,128)(2,1)S(1)} %fusion), channel_id=1, source_target_pairs={{0,1},{1,0},{2,3},{3,2},{4,5},{5,4},{6,7},{7,6},{8,9},{9,8},{10,11... | collective-permute-start | bytes 3145736 | tf_op jit(solution)/shard_map/ppermute | solution.py:139
where the time goes:
time: 92 us; the launch traced here: 91.7 us
  Pallas kernels  52.4 us (57%)
  waiting for transfers between devices  22 us (24%)
  starting transfers between devices  8.81 us (10%)
  local copies, waits for them, and re-layouts  7.33 us (8%)
  other arithmetic  1.09 us (1%)
    pallas_call x2, Pallas kernels, shards(): pl.pallas_call(functools.partial(transform_kernel, parts, frames, rows, d...  38 us
    ppermute x2, waiting for transfers between devices, sent(): return lax.ppermute(narrow, 'tm', route).astype(jnp.float32) * 0.5  16.8 us
    pallas_call x2, Pallas kernels, shards(): pl.pallas_call(functools.partial(finish_kernel, parts, frames, rows, step...  14.4 us
    ppermute x2, starting transfers between devices, shards(): lax.ppermute(x[s:s + 1, :, frames - depth:], 'tm', route)  6.19 us
    reshape x1, local copies, waits for them, and re-layouts, shards(): x = signal.reshape(streams, 2, frames, rows, LANES)  6.11 us
    ppermute x2, waiting for transfers between devices, shards(): lax.ppermute(x[s:s + 1, :, frames - depth:], 'tm', route)  5.22 us
    ppermute x2, starting transfers between devices, sent(): return lax.ppermute(narrow, 'tm', route).astype(jnp.float32) * 0.5  2.62 us
  transfers between devices with their start and end apart: 4, of which 3 were waited for; matrix products, arithmetic and copies ran while one was open for 1% of the time, Pallas kernels for 49%

commit v1 on v0

v1 whole, which is shorter than its diff:
```python
import functools
import math

import jax
import jax.numpy as jnp
import numpy as np
from jax import lax
from jax.experimental import pallas as pl
from jax.experimental.pallas import tpu as pltpu
from jax.sharding import PartitionSpec as P

LANES = 128
GROUP = 4
BATCH = 2 * GROUP
PAIR = 2
POWER = 6
SCALE = 64.0


def angles(height, breadth, modulus):
    product = np.arange(height)[:, None] * np.arange(breadth)[None, :] % modulus
    return product * (2.0 * math.pi / modulus)


def split(table):
    high = table.astype(np.float32).astype(jnp.bfloat16)
    low = (table - high.astype(np.float64)).astype(np.float32).astype(jnp.bfloat16)
    return high, low


def first_table(rows):
    turn = angles(rows, rows, rows)
    cos, sin = np.cos(turn), np.sin(turn)
    whole = np.block([[cos, sin], [-sin, cos]])
    woven = whole.reshape(2 * rows, 2, rows).transpose(0, 2, 1).reshape(2 * rows, 2 * rows)
    high, low = split(np.kron(np.eye(GROUP), woven))
    return np.concatenate([high, low, high], axis=1)


def second_table(channels, parts):
    turn = angles(LANES, LANES, LANES)
    scale = 1.0 / math.isqrt(channels)
    cos, sin = np.cos(turn) * scale, np.sin(turn) * scale
    each = LANES // parts
    blocks = []
    for part in range(parts):
        pick = slice(part * each, (part + 1) * each)
        blocks.append(np.block([[cos[pick], sin[pick]], [-sin[pick], cos[pick]]]))
    high, low = split(np.concatenate(blocks, axis=0))
    table = np.concatenate([high, low, high], axis=1)
    return np.concatenate([table, table], axis=0)


def encode(value):
    value = value * SCALE
    square = value * jnp.abs(value)
    return (square * (square * square)).astype(jnp.bfloat16)


def decode(code):
    value = code.astype(jnp.float32)
    size = jnp.exp(jnp.log(jnp.abs(value)) * (1.0 / POWER)) * (1.0 / SCALE)
    return jnp.where(value < 0.0, -size, size)


def halves(value):
    high = value.astype(jnp.bfloat16)
    low = (value - high.astype(jnp.float32)).astype(jnp.bfloat16)
    return high, low


def channelize(parts, streams, frames, rows, depth, x_hbm, taps_ref, first_ref, cos_ref, sin_ref,
               second_ref, out_ref, xbuf, halo, wide, grid, zr, zi, own, send, recv,
               x_sem, halo_send, halo_recv, send_sem, recv_sem):
    me = lax.axis_index("tm")
    each = LANES // parts
    past = depth - 1
    pitch = zr.shape[0] // rows
    steps = rows // PAIR

    barrier = pltpu.get_barrier_semaphore()
    for k in range(1, parts):
        pl.semaphore_signal(barrier, inc=1, device_id={"tm": lax.rem(me + k, parts)},
                            device_id_type=pl.DeviceIdType.MESH)
    load = pltpu.make_async_copy(x_hbm.at[0], xbuf, x_sem)
    load.start()
    pl.semaphore_wait(barrier, parts - 1)

    def edge(s):
        return pltpu.make_async_remote_copy(
            src_ref=x_hbm.at[s, pl.ds(frames - past, past)], dst_ref=halo.at[s],
            send_sem=halo_send.at[s], recv_sem=halo_recv.at[s],
            device_id={"tm": lax.rem(me + 1, parts)}, device_id_type=pl.DeviceIdType.MESH)

    def piece(s, k, step):
        return pltpu.make_async_remote_copy(
            src_ref=send.at[s, k - 1, step], dst_ref=recv.at[s, k - 1, step],
            send_sem=send_sem.at[s, k - 1, step], recv_sem=recv_sem.at[s, k - 1, step],
            device_id={"tm": lax.rem(me + k, parts)}, device_id_type=pl.DeviceIdType.MESH)

    @pl.when(me < parts - 1)
    def _():
        for s in range(streams):
            edge(s).start()

    def first_stage(step):
        base = pl.multiple_of(step * BATCH, BATCH)
        for block in range(2 * rows // 8):
            sub = slice(block * 8, block * 8 + 8)
            data = [wide[base + i, sub, :] for i in range(BATCH + past)]
            taps = [taps_ref[k, sub, :] for k in range(depth)]
            for t in range(BATCH):
                total = taps[0] * data[t + past]
                for k in range(1, depth):
                    total = total + taps[k] * data[t + past - k]
                row = (t % GROUP) * 2 * rows + block * 8
                lane = (t // GROUP) * LANES
                grid[row : row + 8, lane : lane + LANES] = total
        high, low = halves(grid[...])
        out = jnp.dot(first_ref[...], jnp.concatenate([high, high, low], axis=0),
                      preferred_element_type=jnp.float32)
        cos, sin = cos_ref[...], sin_ref[...]
        for t in range(BATCH):
            row = (t % GROUP) * 2 * rows
            lane = (t // GROUP) * LANES
            real = out[row : row + rows, lane : lane + LANES]
            imag = out[row + rows : row + 2 * rows, lane : lane + LANES]
            pick = pl.ds(base + t, rows, stride=pitch)
            zr[pick, :] = real * cos + imag * sin
            zi[pick, :] = imag * cos - real * sin

    def second_stage(s, step):
        pieces = []
        for i in range(PAIR):
            pick = pl.ds(pl.multiple_of((step * PAIR + i) * pitch, 8), frames)
            pieces.append(jnp.concatenate([zr[pick, :], zi[pick, :]], axis=1))
        high, low = halves(jnp.concatenate(pieces, axis=0))
        top = pl.ds(pl.multiple_of(me * 2 * each, 2 * each), 2 * LANES)
        out = lax.dot_general(second_ref[top, :], jnp.concatenate([high, high, low], axis=1),
                              (((1,), (1,)), ((), ())), preferred_element_type=jnp.float32)
        for i in range(PAIR):
            lane = slice(i * frames, (i + 1) * frames)
            for p in range(2):
                own[s, p, step * PAIR + i] = out[p * each : (p + 1) * each, lane]
                for k in range(1, parts):
                    row = (2 * k + p) * each
                    send[s, k - 1, step, p, i] = encode(out[row : row + each, lane])

    def finish(s, step):
        for k in range(1, parts):
            piece(s, k, step).wait_recv()
        for i in range(PAIR):
            c = step * PAIR + i
            data = [[own[s, p, c] for p in range(2)]]
            for k in range(1, parts):
                data.append([decode(recv[s, k - 1, step, p, i]) for p in range(2)])
            square = sum(d[0] * d[0] + d[1] * d[1] for d in data)
            power = jnp.sum(square, axis=1, keepdims=True)
            factor = lax.rsqrt(power * (1.0 / (frames * parts)) + 1.0)
            for k in range(parts):
                source = lax.rem(me + parts - k, parts) * (frames // LANES)
                for p in range(2):
                    result = data[k][p] * factor
                    for j in range(frames // LANES):
                        lane = slice(j * LANES, (j + 1) * LANES)
                        out_ref[s, p, source + j, pl.ds(c, each, stride=rows), :] = result[:, lane]

    for s in range(streams):
        load.wait()

        @pl.loop(0, frames // BATCH)
        def _(step):
            base = pl.multiple_of(step * BATCH, BATCH)
            wide[pl.ds(base + past, BATCH)] = xbuf[pl.ds(base, BATCH)].astype(jnp.float32)

        if s + 1 < streams:
            load = pltpu.make_async_copy(x_hbm.at[s + 1], xbuf, x_sem)
            load.start()

        front = -(-past // BATCH)

        @pl.loop(front, frames // BATCH)
        def _(step):
            first_stage(step)

        @pl.when(me > 0)
        def _():
            edge(s).wait_recv()
            wide[:past] = halo[s].astype(jnp.float32)

        @pl.when(me == 0)
        def _():
            wide[:past] = jnp.zeros((past, 2 * rows, LANES), jnp.float32)

        @pl.loop(0, front)
        def _(step):
            first_stage(step)

        @pl.loop(0, steps)
        def _(step):
            second_stage(s, step)

            @pl.when(step > 0)
            def _():
                for k in range(1, parts):
                    piece(s, k, step - 1).start()

        for k in range(1, parts):
            piece(s, k, steps - 1).start()

    for s in range(streams):

        @pl.loop(0, steps)
        def _(step):
            finish(s, step)

    for s in range(streams):

        @pl.loop(0, steps)
        def _(step):
            for k in range(1, parts):
                piece(s, k, step).wait_send()

    @pl.when(me < parts - 1)
    def _():
        for s in range(streams):
            edge(s).wait_send()


def deliver(streams, spans, planes_ref, out_ref, sem):
    copies = []
    for s in range(streams):
        for p in range(2):
            for j in range(spans):
                lane = slice(j * LANES, (j + 1) * LANES)
                copies.append(pltpu.make_async_copy(
                    planes_ref.at[s, p, j], out_ref.at[s, p, :, lane], sem.at[s, p, j]))
    for copy in copies:
        copy.start()
    for copy in copies:
        copy.wait()


def shards(parts, signal, taps):
    streams = signal.shape[0]
    depth, channels = taps.shape
    rows = channels // LANES
    frames = signal.shape[2] // channels
    each = LANES // parts
    chunks = signal.shape[2] // LANES
    x = signal.reshape(streams, 2, chunks, LANES).transpose(0, 2, 1, 3)
    x = x.reshape(streams, frames, 2 * rows, LANES)
    taps = jnp.repeat(taps.reshape(depth, rows, LANES), 2, axis=1)
    twist = angles(rows, LANES, channels)
    cos, sin = jnp.asarray(np.cos(twist), jnp.float32), jnp.asarray(np.sin(twist), jnp.float32)
    first = jnp.asarray(first_table(rows))
    second = jnp.asarray(second_table(channels, parts))
    steps = rows // PAIR
    pitch = frames + 8
    vmem = pl.BlockSpec(memory_space=pltpu.VMEM)
    code = (streams, parts - 1, steps, 2, PAIR, each, frames)
    spans = frames * parts // LANES
    width = 2 * rows * LANES * frames
    limit = (8 << 20) + 2 * width + 4 * width + 4 * width * 9 // 8 + 8 * width * streams * (parts + 1) // parts
    planes = pl.pallas_call(
        functools.partial(channelize, parts, streams, frames, rows, depth),
        in_specs=[pl.BlockSpec(memory_space=pl.ANY)] + [vmem] * 5,
        out_specs=vmem,
        out_shape=jax.ShapeDtypeStruct((streams, 2, spans, channels // parts, LANES), jnp.float32),
        scratch_shapes=[
            pltpu.VMEM((frames, 2 * rows, LANES), jnp.bfloat16),
            pltpu.VMEM((streams, depth - 1, 2 * rows, LANES), jnp.bfloat16),
            pltpu.VMEM((depth - 1 + frames, 2 * rows, LANES), jnp.float32),
            pltpu.VMEM((2 * GROUP * rows, 2 * LANES), jnp.float32),
            pltpu.VMEM((rows * pitch, LANES), jnp.float32),
            pltpu.VMEM((rows * pitch, LANES), jnp.float32),
            pltpu.VMEM((streams, 2, rows, each, frames), jnp.float32),
            pltpu.VMEM(code, jnp.bfloat16),
            pltpu.VMEM(code, jnp.bfloat16),
            pltpu.SemaphoreType.DMA,
            pltpu.SemaphoreType.DMA((streams,)),
            pltpu.SemaphoreType.DMA((streams,)),
            pltpu.SemaphoreType.DMA((streams, parts - 1, steps)),
            pltpu.SemaphoreType.DMA((streams, parts - 1, steps)),
        ],
        compiler_params=pltpu.CompilerParams(
            vmem_limit_bytes=limit, collective_id=0, has_side_effects=True),
        cost_estimate=pl.CostEstimate(flops=16 * 10**9, bytes_accessed=16 << 20, transcendentals=0),
        name="channelize",
    )(x, taps, first, cos, sin, second)
    return pl.pallas_call(
        functools.partial(deliver, streams, spans),
        in_specs=[vmem],
        out_specs=pl.BlockSpec(memory_space=pl.ANY),
        out_shape=jax.ShapeDtypeStruct((streams, 2, channels // parts, spans * LANES), jnp.float32),
        scratch_shapes=[pltpu.SemaphoreType.DMA((streams, 2, spans))],
        compiler_params=pltpu.CompilerParams(vmem_limit_bytes=20 << 20),
        cost_estimate=pl.CostEstimate(flops=10**6, bytes_accessed=16 << 20, transcendentals=0),
        name="deliver",
    )(planes)


def solution(mesh):
    in_specs = (P("stream", None, "tm"), P())
    out_specs = P("stream", None, "tm", None)
    body = functools.partial(shards, mesh.shape["tm"])
    return jax.shard_map(body, mesh=mesh, in_specs=in_specs, out_specs=out_specs, check_vma=False)
```

time: 92 us -> 77.3 us (0.84)
  waiting for transfers between devices: 22 us -> 0 us
  Pallas kernels: 52.4 us -> 66.5 us
  starting transfers between devices: 8.81 us -> 0 us
  local copies, waits for them, and re-layouts: 7.33 us -> 10.3 us
  other arithmetic: 1.09 us -> 0 us
    ppermute x4 -> x0, waiting for transfers between devices: 22 us -> none  [the longest x2 16.8 us: sent(): return lax.ppermute(narrow, 'tm', route).astype(jnp.float32) * 0.5]
    pallas_call x4 -> x2, Pallas kernels: 52.4 us -> 66.5 us  [the longest x1 63.2 us: shards(): pl.pallas_call(functools.partial(channelize, parts, streams, frames, rows...]
    unnamed x11 -> x13, local copies, waits for them, and re-layouts: 0.07 us -> 10.1 us
    ppermute x4 -> x0, starting transfers between devices: 8.81 us -> none  [the longest x2 6.19 us: shards(): lax.ppermute(x[s:s + 1, :, frames - depth:], 'tm', route)]
    reshape x1 -> x0, local copies, waits for them, and re-layouts: 6.11 us -> none  [shards(): x = signal.reshape(streams, 2, frames, rows, LANES)]
    slice x1 -> x0, local copies, waits for them, and re-layouts: 1.12 us -> none  [shards(): x[s:s + 1, :, frames - depth:]]
  transfers between devices with their start and end apart: 4 -> 0, of which waited for: 3 -> 0; matrix products, arithmetic and copies ran while one was open for 1% -> 0% of each run, Pallas kernels for 49% -> 0%
where the time goes in v1:
time: 77.3 us; the launch traced here: 76.9 us
  Pallas kernels  66.5 us (86%)
  local copies, waits for them, and re-layouts  10.3 us (13%)
    pallas_call x1, Pallas kernels, shards(): pl.pallas_call(functools.partial(channelize, parts, streams, frames, rows...  63.2 us
    unnamed x13, local copies, waits for them, and re-layouts  10.1 us
    pallas_call x1, Pallas kernels, shards(): pl.pallas_call(functools.partial(deliver, streams, spans), in_specs=[vmem...  3.36 us

profile of v1, /device:TPU:0, one launch (start us, length us, event | category | flops | bytes accessed | tf_op | source)
XLA Modules:
  0.0 76.9 jit_solution(9858983514804089560)
XLA Ops:
  0.0 1.0 %copy.8 = f32[2,8,32,128]{3,2,1,0:T(8,128)S(1)} copy(f32[2,8,32,128]{3,1,2,0:T(8,128)} %bitcast.11) | data formatting | bytes 524288
  1.0 0.2 broadcast_in_dim.3
  1.2 0.0 copy-start.1
  1.2 2.2 %copy-done.1 = bf16[2,2,524288]{2,1,0:T(2,128)(2,1)S(1)} copy-done((bf16[2,2,524288]{2,1,0:T(2,128)(2,1)S(1)}, bf16[2,2,524288]{2,1,0:T(2,128)(2,1)}, u32[]{:S(2)}) %copy-start.1) | copy-done | bytes 4194328
  3.4 0.0 copy-start.2
  3.4 1.1 %copy-done.2 = bf16[512,768]{1,0:T(8,128)(2,1)S(1)} copy-done((bf16[512,768]{1,0:T(8,128)(2,1)S(1)}, bf16[512,768]{1,0:T(8,128)(2,1)}, u32[]{:S(2)}) %copy-start.2) | copy-done | bytes 786456
  4.5 0.0 copy-start.3
  4.5 1.0 %copy-done.3 = bf16[256,768]{1,0:T(8,128)(2,1)S(1)} copy-done((bf16[256,768]{1,0:T(8,128)(2,1)S(1)}, bf16[256,768]{1,0:T(8,128)(2,1)}, u32[]{:S(2)}) %copy-start.3) | copy-done | bytes 393240
  5.5 0.0 copy-start.4
  5.5 0.7 copy-done.4
  6.2 0.0 copy-start.5
  6.2 0.7 copy-done.5
  7.0 63.2 %channelize.1.planes_ref = f32[2,2,2,2048,128]{4,3,2,1,0:T(8,128)} custom-call(bf16[2,128,64,128]{3,2,1,0:T(8,128)(2,1)S(1)} %bitcast.9, f32[16,64,128]{2,1,0:T(8,128)S(1)} %bitcast.8, bf16[256,768]{1,0:T(8,128)(2,1)S(1)} %copy-done.3, f32[32,128]{1,0:T(8,128)S(1)} %copy-done.5, f32[32,128]{1,0:T(8,128)S(1)} %copy-done.4, bf16[512,768]{1,0:T(8,128)(2,1)S(1)} %copy-done.2), custom_call_target="tpu_custom_call" | custom-call | flops 16000000000 | bytes 16777216 | tf_op jit(solution)/shard_map/channelize/pallas_call | solution.py:265
  70.1 0.0 copy-start
  70.1 3.4 %copy-done = f32[2,2,2,2048,128]{4,3,2,1,0:T(8,128)S(1)} copy-done((f32[2,2,2,2048,128]{4,3,2,1,0:T(8,128)S(1)}, f32[2,2,2,2048,128]{4,3,2,1,0:T(8,128)}, u32[]{:S(2)}) %copy-start) | copy-done | bytes 8388632
  73.5 3.4 %deliver.1 = f32[2,2,2048,256]{3,2,1,0:T(8,128)} custom-call(f32[2,2,2,2048,128]{4,3,2,1,0:T(8,128)S(1)} %copy-done), custom_call_target="tpu_custom_call" | custom-call | flops 1000000 | bytes 16777216 | tf_op jit(solution)/shard_map/deliver/pallas_call | solution.py:291
Async XLA Ops:
  1.2 2.2 %copy-start.1 = (bf16[2,2,524288]{2,1,0:T(2,128)(2,1)S(1)}, bf16[2,2,524288]{2,1,0:T(2,128)(2,1)}, u32[]{:S(2)}) copy-start(bf16[2,2,524288]{2,1,0:T(2,128)(2,1)} %param.6) | copy-start | bytes 12582916
  3.4 1.1 %copy-start.2 = (bf16[512,768]{1,0:T(8,128)(2,1)S(1)}, bf16[512,768]{1,0:T(8,128)(2,1)}, u32[]{:S(2)}) copy-start(bf16[512,768]{1,0:T(8,128)(2,1)} %constant.11.clone.second_ref) | copy-start | bytes 2359300
  4.5 1.0 %copy-start.3 = (bf16[256,768]{1,0:T(8,128)(2,1)S(1)}, bf16[256,768]{1,0:T(8,128)(2,1)}, u32[]{:S(2)}) copy-start(bf16[256,768]{1,0:T(8,128)(2,1)} %constant.10.clone.first_ref) | copy-start | bytes 1179652
  5.5 0.7 copy-start.4
  6.2 0.7 copy-start.5
  70.1 3.4 %copy-start = (f32[2,2,2,2048,128]{4,3,2,1,0:T(8,128)S(1)}, f32[2,2,2,2048,128]{4,3,2,1,0:T(8,128)}, u32[]{:S(2)}) copy-start(f32[2,2,2,2048,128]{4,3,2,1,0:T(8,128)} %channelize.1.planes_ref) | copy-start | bytes 25165828

commit v2 on v1

--- a/solution.py
+++ b/solution.py
@@ -69,14 +69,17 @@
     return high, low
 
 
-def channelize(parts, streams, frames, rows, depth, x_hbm, taps_ref, first_ref, cos_ref, sin_ref,
-               second_ref, out_ref, xbuf, halo, wide, grid, zr, zi, own, send, recv,
-               x_sem, halo_send, halo_recv, send_sem, recv_sem):
+def channelize(parts, streams, frames, rows, depth, x_hbm, taps_hbm, first_hbm, cos_hbm, sin_hbm,
+               second_hbm, out_ref, xbuf, taps_raw, taps_ref, first_ref, cos_ref, sin_ref, second_ref,
+               halo, wide, grid, zr, zi, own, send, recv,
+               x_sem, table_sem, halo_send, halo_recv, send_sem, recv_sem):
     me = lax.axis_index("tm")
     each = LANES // parts
     past = depth - 1
     pitch = zr.shape[0] // rows
     steps = rows // PAIR
+    spans = frames * parts // LANES
+    reach = taps_ref.shape[0] // depth
 
     barrier = pltpu.get_barrier_semaphore()
     for k in range(1, parts):
@@ -84,6 +87,14 @@
                             device_id_type=pl.DeviceIdType.MESH)
     load = pltpu.make_async_copy(x_hbm.at[0], xbuf, x_sem)
     load.start()
+    tables = [
+        pltpu.make_async_copy(source, target, table_sem.at[i])
+        for i, (source, target) in enumerate([
+            (taps_hbm, taps_raw), (first_hbm, first_ref), (cos_hbm, cos_ref),
+            (sin_hbm, sin_ref), (second_hbm, second_ref)])
+    ]
+    for table in tables:
+        table.start()
     pl.semaphore_wait(barrier, parts - 1)
 
     def edge(s):
@@ -103,12 +114,22 @@
         for s in range(streams):
             edge(s).start()
 
+    for table in tables:
+        table.wait()
+
+    @pl.loop(0, rows)
+    def _(n):
+        for g in range(depth // 8):
+            for p in range(2):
+                row = pl.ds(g * 8 * reach + 2 * n + p, 8, stride=reach)
+                taps_ref[row, :] = taps_raw[g, n]
+
     def first_stage(step):
         base = pl.multiple_of(step * BATCH, BATCH)
         for block in range(2 * rows // 8):
             sub = slice(block * 8, block * 8 + 8)
             data = [wide[base + i, sub, :] for i in range(BATCH + past)]
-            taps = [taps_ref[k, sub, :] for k in range(depth)]
+            taps = [taps_ref[k * reach + block * 8 : k * reach + block * 8 + 8, :] for k in range(depth)]
             for t in range(BATCH):
                 total = taps[0] * data[t + past]
                 for k in range(1, depth):
@@ -159,11 +180,13 @@
             factor = lax.rsqrt(power * (1.0 / (frames * parts)) + 1.0)
             for k in range(parts):
                 source = lax.rem(me + parts - k, parts) * (frames // LANES)
+                top = (c // 8) * (8 * spans) + c % 8
                 for p in range(2):
                     result = data[k][p] * factor
                     for j in range(frames // LANES):
                         lane = slice(j * LANES, (j + 1) * LANES)
-                        out_ref[s, p, source + j, pl.ds(c, each, stride=rows), :] = result[:, lane]
+                        row = pl.ds(top + (source + j) * 8, each, stride=rows * spans)
+                        out_ref[s, p, row, :] = result[:, lane]
 
     for s in range(streams):
         load.wait()
@@ -225,20 +248,6 @@
     def _():
         for s in range(streams):
             edge(s).wait_send()
-
-
-def deliver(streams, spans, planes_ref, out_ref, sem):
-    copies = []
-    for s in range(streams):
-        for p in range(2):
-            for j in range(spans):
-                lane = slice(j * LANES, (j + 1) * LANES)
-                copies.append(pltpu.make_async_copy(
-                    planes_ref.at[s, p, j], out_ref.at[s, p, :, lane], sem.at[s, p, j]))
-    for copy in copies:
-        copy.start()
-    for copy in copies:
-        copy.wait()
 
 
 def shards(parts, signal, taps):
@@ -250,25 +259,35 @@
     chunks = signal.shape[2] // LANES
     x = signal.reshape(streams, 2, chunks, LANES).transpose(0, 2, 1, 3)
     x = x.reshape(streams, frames, 2 * rows, LANES)
-    taps = jnp.repeat(taps.reshape(depth, rows, LANES), 2, axis=1)
+    taps = taps.reshape(depth // 8, 8, rows, LANES).transpose(0, 2, 1, 3)
     twist = angles(rows, LANES, channels)
     cos, sin = jnp.asarray(np.cos(twist), jnp.float32), jnp.asarray(np.sin(twist), jnp.float32)
     first = jnp.asarray(first_table(rows))
     second = jnp.asarray(second_table(channels, parts))
     steps = rows // PAIR
     pitch = frames + 8
-    vmem = pl.BlockSpec(memory_space=pltpu.VMEM)
-    code = (streams, parts - 1, steps, 2, PAIR, each, frames)
+    reach = 2 * rows + 8
     spans = frames * parts // LANES
+    tiles = channels // parts // 8
     width = 2 * rows * LANES * frames
     limit = (8 << 20) + 2 * width + 4 * width + 4 * width * 9 // 8 + 8 * width * streams * (parts + 1) // parts
-    planes = pl.pallas_call(
+    hbm = pl.BlockSpec(memory_space=pltpu.HBM)
+    code = (streams, parts - 1, steps, 2, PAIR, each, frames)
+    operands = [x, taps, first, cos, sin, second]
+    operands = [pltpu.with_memory_space_constraint(a, pltpu.HBM) for a in operands]
+    out = pl.pallas_call(
         functools.partial(channelize, parts, streams, frames, rows, depth),
-        in_specs=[pl.BlockSpec(memory_space=pl.ANY)] + [vmem] * 5,
-        out_specs=vmem,
-        out_shape=jax.ShapeDtypeStruct((streams, 2, spans, channels // parts, LANES), jnp.float32),
+        in_specs=[hbm] * 6,
+        out_specs=pl.BlockSpec(memory_space=pltpu.VMEM),
+        out_shape=pltpu.VMEM((streams, 2, 8 * tiles * spans, LANES), jnp.float32),
         scratch_shapes=[
             pltpu.VMEM((frames, 2 * rows, LANES), jnp.bfloat16),
+            pltpu.VMEM(taps.shape, jnp.float32),
+            pltpu.VMEM((depth * reach, LANES), jnp.float32),
+            pltpu.VMEM(first.shape, jnp.bfloat16),
+            pltpu.VMEM(cos.shape, jnp.float32),
+            pltpu.VMEM(sin.shape, jnp.float32),
+            pltpu.VMEM(second.shape, jnp.bfloat16),
             pltpu.VMEM((streams, depth - 1, 2 * rows, LANES), jnp.bfloat16),
             pltpu.VMEM((depth - 1 + frames, 2 * rows, LANES), jnp.float32),
             pltpu.VMEM((2 * GROUP * rows, 2 * LANES), jnp.float32),
@@ -278,6 +297,7 @@
             pltpu.VMEM(code, jnp.bfloat16),
             pltpu.VMEM(code, jnp.bfloat16),
             pltpu.SemaphoreType.DMA,
+            pltpu.SemaphoreType.DMA((5,)),
             pltpu.SemaphoreType.DMA((streams,)),
             pltpu.SemaphoreType.DMA((streams,)),
             pltpu.SemaphoreType.DMA((streams, parts - 1, steps)),
@@ -287,17 +307,9 @@
             vmem_limit_bytes=limit, collective_id=0, has_side_effects=True),
         cost_estimate=pl.CostEstimate(flops=16 * 10**9, bytes_accessed=16 << 20, transcendentals=0),
         name="channelize",
-    )(x, taps, first, cos, sin, second)
-    return pl.pallas_call(
-        functools.partial(deliver, streams, spans),
-        in_specs=[vmem],
-        out_specs=pl.BlockSpec(memory_space=pl.ANY),
-        out_shape=jax.ShapeDtypeStruct((streams, 2, channels // parts, spans * LANES), jnp.float32),
-        scratch_shapes=[pltpu.SemaphoreType.DMA((streams, 2, spans))],
-        compiler_params=pltpu.CompilerParams(vmem_limit_bytes=20 << 20),
-        cost_estimate=pl.CostEstimate(flops=10**6, bytes_accessed=16 << 20, transcendentals=0),
-        name="deliver",
-    )(planes)
+    )(*operands)
+    out = out.reshape(streams, 2, tiles, spans, 8, LANES).transpose(0, 1, 2, 4, 3, 5)
+    return out.reshape(streams, 2, 8 * tiles, spans * LANES)
 
 
 def solution(mesh):

time: 77.3 us -> 65.3 us (0.84)
  local copies, waits for them, and re-layouts: 10.3 us -> 3.4 us
  Pallas kernels: 66.5 us -> 61.7 us
    unnamed x13 -> x1, local copies, waits for them, and re-layouts: 10.1 us -> 3.4 us
    pallas_call x1 -> x0, Pallas kernels: 3.36 us -> none  [shards(): pl.pallas_call(functools.partial(deliver, streams, spans), in_specs=[vmem...]
    pallas_call x1, Pallas kernels: 63.2 us -> 61.7 us  [shards(): pl.pallas_call(functools.partial(channelize, parts, streams, frames, rows...]
where the time goes in v2:
time: 65.3 us; the launch traced here: 65.1 us
  Pallas kernels  61.7 us (94%)
  local copies, waits for them, and re-layouts  3.4 us (5%)
    pallas_call x1, Pallas kernels, shards(): pl.pallas_call(functools.partial(channelize, parts, streams, frames, rows...  61.7 us
    unnamed x1, local copies, waits for them, and re-layouts  3.4 us

profile of v2, /device:TPU:0, one launch (start us, length us, event | category | flops | bytes accessed | tf_op | source)
XLA Modules:
  0.0 65.1 jit_solution(6512533400673899418)
XLA Ops:
  0.0 61.7 %channelize.1 = f32[2,2,4096,128]{3,2,1,0:T(8,128)S(1)} custom-call(bf16[2,128,64,128]{3,2,1,0:T(8,128)(2,1)} %bitcast.14, f32[2,32,8,128]{3,2,1,0:T(8,128)} %bitcast.15, bf16[256,768]{1,0:T(8,128)(2,1)} %constant.10.clone.first_hbm, f32[32,128]{1,0:T(8,128)} %constant.8.clone.cos_hbm, f32[32,128]{1,0:T(8,128)} %constant.9.clone.sin_hbm, ...), custom_call_target="tpu_custom_call" | custom-call | flops 16000000000 | bytes 16777216 | tf_op jit(solution)/shard_map/channelize/pallas_call | solution.py:278
  61.7 3.4 %copy.9 = f32[2,2,2048,256]{3,2,1,0:T(8,128)} copy(f32[2,2,2048,256]{3,2,1,0:T(8,128)S(1)} %bitcast.13) | data formatting | bytes 16777216

commit v3 on v2

v3 whole, which is shorter than its diff:
```python
import functools
import math

import jax
import jax.numpy as jnp
import numpy as np
from jax import lax
from jax.experimental import pallas as pl
from jax.experimental.pallas import tpu as pltpu
from jax.sharding import PartitionSpec as P

LANES = 128
GROUP = 4
BATCH = 2 * GROUP
SPAN = 64
WIDE = 2 * LANES
POWER = 6
SCALE = 64.0


def angles(height, breadth, modulus):
    product = np.arange(height)[:, None] * np.arange(breadth)[None, :] % modulus
    return product * (2.0 * math.pi / modulus)


def split(table):
    high = table.astype(np.float32).astype(jnp.bfloat16)
    low = (table - high.astype(np.float64)).astype(np.float32).astype(jnp.bfloat16)
    return high, low


def first_table(rows):
    turn = angles(rows, rows, rows)
    cos, sin = np.cos(turn), np.sin(turn)
    whole = np.block([[cos, sin], [-sin, cos]])
    woven = whole.reshape(2 * rows, 2, rows).transpose(0, 2, 1).reshape(2 * rows, 2 * rows)
    high, low = split(np.kron(np.eye(GROUP), woven))
    return np.concatenate([high, low, high], axis=1)


def second_table(channels, parts):
    turn = angles(LANES, LANES, LANES)
    scale = 1.0 / math.isqrt(channels)
    cos, sin = np.cos(turn) * scale, np.sin(turn) * scale
    each = LANES // parts
    blocks = []
    for part in range(parts):
        pick = slice(part * each, (part + 1) * each)
        blocks.append(np.block([[cos[pick], sin[pick]], [-sin[pick], cos[pick]]]))
    high, low = split(np.concatenate(blocks, axis=0))
    table = np.concatenate([high, low, high], axis=1)
    return np.concatenate([table, table], axis=0)


def encode(value):
    value = value * SCALE
    square = value * jnp.abs(value)
    return (square * (square * square)).astype(jnp.bfloat16)


def decode(code):
    value = code.astype(jnp.float32)
    size = jnp.exp(jnp.log(jnp.abs(value)) * (1.0 / POWER)) * (1.0 / SCALE)
    return jnp.where(value < 0.0, -size, size)


def halves(value):
    high = value.astype(jnp.bfloat16)
    low = (value - high.astype(jnp.float32)).astype(jnp.bfloat16)
    return high, low


def channelize(parts, streams, frames, rows, depth, x_hbm, taps_hbm, first_hbm, cos_hbm, sin_hbm,
               second_hbm, out_ref, xbuf, taps_raw, taps_ref, first_ref, cos_ref, sin_ref, second_ref,
               halo, wide, grid, zr, zi, own, send, recv, own_over, send_over, recv_over,
               x_sem, table_sem, halo_send, halo_recv, send_sem, recv_sem, over_send, over_recv):
    me = lax.axis_index("tm")
    each = LANES // parts
    past = depth - 1
    over = -(-past // BATCH) * BATCH
    blocks = frames // SPAN
    quad = WIDE // SPAN
    steps = rows // quad
    group = WIDE // over
    spans = frames * parts // LANES
    reach = taps_ref.shape[0] // depth
    bounds = [max(b * SPAN - over, 0) for b in range(blocks)] + [frames]

    barrier = pltpu.get_barrier_semaphore()
    for k in range(1, parts):
        pl.semaphore_signal(barrier, inc=1, device_id={"tm": lax.rem(me + k, parts)},
                            device_id_type=pl.DeviceIdType.MESH)

    def load(s, b):
        pick = pl.ds(bounds[b], bounds[b + 1] - bounds[b])
        return pltpu.make_async_copy(x_hbm.at[s, pick], xbuf.at[pick], x_sem.at[b])

    def edge():
        return pltpu.make_async_remote_copy(
            src_ref=x_hbm.at[0, pl.ds(frames - past, past)], dst_ref=halo,
            send_sem=halo_send, recv_sem=halo_recv,
            device_id={"tm": lax.rem(me + 1, parts)}, device_id_type=pl.DeviceIdType.MESH)

    def piece(s, k, b, step):
        return pltpu.make_async_remote_copy(
            src_ref=send.at[s, k - 1, b, step], dst_ref=recv.at[s, k - 1, b, step],
            send_sem=send_sem.at[s, k - 1, b, step], recv_sem=recv_sem.at[s, k - 1, b, step],
            device_id={"tm": lax.rem(me + k, parts)}, device_id_type=pl.DeviceIdType.MESH)

    def overhang(s, k):
        return pltpu.make_async_remote_copy(
            src_ref=send_over.at[s - 1, k - 1], dst_ref=recv_over.at[s - 1, k - 1],
            send_sem=over_send.at[s - 1, k - 1], recv_sem=over_recv.at[s - 1, k - 1],
            device_id={"tm": lax.rem(me + k, parts)}, device_id_type=pl.DeviceIdType.MESH)

    load(0, blocks - 1).start()
    tables = [
        pltpu.make_async_copy(source, target, table_sem.at[i])
        for i, (source, target) in enumerate([
            (taps_hbm, taps_raw), (first_hbm, first_ref), (cos_hbm, cos_ref),
            (sin_hbm, sin_ref), (second_hbm, second_ref)])
    ]
    for table in tables:
        table.start()
    for b in reversed(range(blocks - 1)):
        load(0, b).start()
    pl.semaphore_wait(barrier, parts - 1)

    @pl.when(me < parts - 1)
    def _():
        edge().start()

    for table in tables:
        table.wait()

    @pl.loop(0, rows)
    def _(n):
        for g in range(depth // 8):
            for p in range(2):
                row = pl.ds(g * 8 * reach + 2 * n + p, 8, stride=reach)
                taps_ref[row, :] = taps_raw[g, n]

    wide[past + frames :] = jnp.zeros((over, 2 * rows, LANES), jnp.float32)

    def widen(s, b):
        load(s, b).wait()

        @pl.loop(bounds[b] // BATCH, bounds[b + 1] // BATCH)
        def _(step):
            base = pl.multiple_of(step * BATCH, BATCH)
            wide[pl.ds(base + past, BATCH)] = xbuf[pl.ds(base, BATCH)].astype(jnp.float32)

    def first_stage(frame, slot, pitch):
        for block in range(2 * rows // 8):
            sub = slice(block * 8, block * 8 + 8)
            data = [wide[frame + i, sub, :] for i in range(BATCH + past)]
            taps = [taps_ref[k * reach + block * 8 : k * reach + block * 8 + 8, :]
                    for k in range(depth)]
            for t in range(BATCH):
                total = taps[0] * data[t + past]
                for k in range(1, depth):
                    total = total + taps[k] * data[t + past - k]
                row = (t % GROUP) * 2 * rows + block * 8
                lane = (t // GROUP) * LANES
                grid[row : row + 8, lane : lane + LANES] = total
        high, low = halves(grid[...])
        out = jnp.dot(first_ref[...], jnp.concatenate([high, high, low], axis=0),
                      preferred_element_type=jnp.float32)
        cos, sin = cos_ref[...], sin_ref[...]
        for t in range(BATCH):
            row = (t % GROUP) * 2 * rows
            lane = (t // GROUP) * LANES
            real = out[row : row + rows, lane : lane + LANES]
            imag = out[row + rows : row + 2 * rows, lane : lane + LANES]
            pick = pl.ds(slot + t, rows, stride=pitch)
            zr[pick, :] = real * cos + imag * sin
            zi[pick, :] = imag * cos - real * sin

    def second_stage(step, count, length, pitch):
        pieces = []
        for i in range(count):
            pick = pl.ds(pl.multiple_of((step * count + i) * pitch, 8), length)
            pieces.append(jnp.concatenate([zr[pick, :], zi[pick, :]], axis=1))
        high, low = halves(jnp.concatenate(pieces, axis=0))
        top = pl.ds(pl.multiple_of(me * 2 * each, 2 * each), 2 * LANES)
        return lax.dot_general(second_ref[top, :], jnp.concatenate([high, high, low], axis=1),
                               (((1,), (1,)), ((), ())), preferred_element_type=jnp.float32)

    def keep(out, mine, theirs):
        for j in range(WIDE // LANES):
            lane = slice(j * LANES, (j + 1) * LANES)
            for p in range(2):
                mine[j, p] = out[p * each : (p + 1) * each, lane]
                for k in range(1, parts):
                    row = (2 * k + p) * each
                    theirs[k - 1][j, p] = encode(out[row : row + each, lane])

    def finish(s, step):
        lanes = lax.broadcasted_iota(jnp.int32, (each, LANES), 1)
        for k in range(1, parts):
            for b in range(blocks):
                piece(s, k, b, step).wait_recv()

        def fetch(k, b, j, p):
            if k == 0:
                return own[s, b, step, j, p]
            return decode(recv[s, k - 1, b, step, j, p])

        def hung(k, c, p):
            at, slot = c // group, (c % group) // (LANES // over)
            if k == 0:
                value = own_over[s - 1, at, slot, p]
            else:
                value = decode(recv_over[s - 1, k - 1, at, slot, p])
            turn = lax.rem(LANES - (c % (LANES // over)) * over, LANES)
            return jnp.where(lanes < over, pltpu.roll(value, turn, 1), 0.0)

        for j in range(WIDE // LANES):
            whole = [[[], []] for _ in range(LANES // SPAN)]
            for k in range(parts):
                for p in range(2):
                    for u in range(frames // LANES):
                        low, high = fetch(k, 2 * u, j, p), fetch(k, 2 * u + 1, j, p)
                        left = lanes < SPAN
                        whole[0][p].append(jnp.where(left, low, pltpu.roll(high, SPAN, 1)))
                        whole[1][p].append(jnp.where(left, pltpu.roll(low, SPAN, 1), high))
            for i in range(LANES // SPAN):
                c = step * quad + j * (LANES // SPAN) + i
                data = whole[i]
                if s > 0:
                    for k in range(parts):
                        source = lax.rem(me + parts - k, parts)
                        for p in range(2):
                            extra = jnp.where(source > 0, hung((k + 1) % parts, c, p), 0.0)
                            at = k * (frames // LANES)
                            data[p][at] = data[p][at] + extra
                square = sum(a * a + b * b for a, b in zip(*data))
                power = jnp.sum(square, axis=1, keepdims=True)
                factor = lax.rsqrt(power * (1.0 / (frames * parts)) + 1.0)
                top = (c // 8) * (8 * spans) + c % 8
                for k in range(parts):
                    source = lax.rem(me + parts - k, parts) * (frames // LANES)
                    for p in range(2):
                        for u in range(frames // LANES):
                            row = pl.ds(top + (source + u) * 8, each, stride=rows * spans)
                            out_ref[s, p, row, :] = data[p][k * (frames // LANES) + u] * factor

    for s in range(streams):
        for b in reversed(range(blocks)):
            widen(s, b)
            if s > 0 and b == blocks - 2:

                @pl.when(me < parts - 1)
                def _():
                    for k in range(1, parts):
                        overhang(s, k).start()

            if b == 0:
                if s + 1 < streams:
                    for n in reversed(range(blocks)):
                        load(s + 1, n).start()
                if s == 0:

                    @pl.when(me > 0)
                    def _():
                        edge().wait_recv()
                        wide[:past] = halo[...].astype(jnp.float32)

                if s == 0:

                    @pl.when(me == 0)
                    def _():
                        wide[:past] = jnp.zeros((past, 2 * rows, LANES), jnp.float32)

                if s == 1:
                    wide[:past] = jnp.zeros((past, 2 * rows, LANES), jnp.float32)

            @pl.loop(0, SPAN // BATCH)
            def _(step):
                base = pl.multiple_of(step * BATCH, BATCH)
                first_stage(b * SPAN + base, base, SPAN + 8)

            @pl.loop(0, steps)
            def _(step):
                out = second_stage(step, quad, SPAN, SPAN + 8)
                keep(out, own.at[s, b, step], [send.at[s, k, b, step] for k in range(parts - 1)])

                @pl.when(step > 0)
                def _():
                    for k in range(1, parts):
                        piece(s, k, b, step - 1).start()

            for k in range(1, parts):
                piece(s, k, b, steps - 1).start()

            if s > 0 and b == blocks - 1:

                @pl.loop(0, over // BATCH)
                def _(step):
                    base = pl.multiple_of(step * BATCH, BATCH)
                    first_stage(frames + base, base, over + 8)

                @pl.loop(0, rows // group)
                def _(step):
                    out = second_stage(step, group, over, over + 8)
                    keep(out, own_over.at[s - 1, step],
                         [send_over.at[s - 1, k, step] for k in range(parts - 1)])

    for s in range(streams):
        if s > 0:
            for k in range(1, parts):

                @pl.when(lax.rem(me + parts - k, parts) < parts - 1)
                def _():
                    overhang(s, k).wait_recv()

        @pl.loop(0, steps)
        def _(step):
            finish(s, step)

    for s in range(streams):

        @pl.loop(0, steps)
        def _(step):
            for k in range(1, parts):
                for b in range(blocks):
                    piece(s, k, b, step).wait_send()

    @pl.when(me < parts - 1)
    def _():
        edge().wait_send()
        for s in range(1, streams):
            for k in range(1, parts):
                overhang(s, k).wait_send()


def shards(parts, signal, taps):
    streams = signal.shape[0]
    depth, channels = taps.shape
    rows = channels // LANES
    frames = signal.shape[2] // channels
    each = LANES // parts
    chunks = signal.shape[2] // LANES
    x = signal.reshape(streams, 2, chunks, LANES).transpose(0, 2, 1, 3)
    x = x.reshape(streams, frames, 2 * rows, LANES)
    taps = taps.reshape(depth // 8, 8, rows, LANES).transpose(0, 2, 1, 3)
    twist = angles(rows, LANES, channels)
    cos, sin = jnp.asarray(np.cos(twist), jnp.float32), jnp.asarray(np.sin(twist), jnp.float32)
    first = jnp.asarray(first_table(rows))
    second = jnp.asarray(second_table(channels, parts))
    blocks = frames // SPAN
    steps = rows * SPAN // WIDE
    over = -(-(depth - 1) // BATCH) * BATCH
    pitch = SPAN + 8
    reach = 2 * rows + 8
    spans = frames * parts // LANES
    tiles = channels // parts // 8
    width = 2 * rows * LANES * frames
    limit = (8 << 20) + 2 * width + 4 * width + 4 * width * 9 // 8 + 8 * width * streams * (parts + 1) // parts
    hbm = pl.BlockSpec(memory_space=pltpu.HBM)
    code = (streams, parts - 1, blocks, steps, WIDE // LANES, 2, each, LANES)
    hung = (streams - 1, parts - 1, rows * over // WIDE, WIDE // LANES, 2, each, LANES)
    operands = [x, taps, first, cos, sin, second]
    operands = [pltpu.with_memory_space_constraint(a, pltpu.HBM) for a in operands]
    out = pl.pallas_call(
        functools.partial(channelize, parts, streams, frames, rows, depth),
        in_specs=[hbm] * 6,
        out_specs=pl.BlockSpec(memory_space=pltpu.VMEM),
        out_shape=pltpu.VMEM((streams, 2, 8 * tiles * spans, LANES), jnp.float32),
        scratch_shapes=[
            pltpu.VMEM((frames, 2 * rows, LANES), jnp.bfloat16),
            pltpu.VMEM(taps.shape, jnp.float32),
            pltpu.VMEM((depth * reach, LANES), jnp.float32),
            pltpu.VMEM(first.shape, jnp.bfloat16),
            pltpu.VMEM(cos.shape, jnp.float32),
            pltpu.VMEM(sin.shape, jnp.float32),
            pltpu.VMEM(second.shape, jnp.bfloat16),
            pltpu.VMEM((depth - 1, 2 * rows, LANES), jnp.bfloat16),
            pltpu.VMEM((depth - 1 + frames + over, 2 * rows, LANES), jnp.float32),
            pltpu.VMEM((2 * GROUP * rows, 2 * LANES), jnp.float32),
            pltpu.VMEM((rows * pitch, LANES), jnp.float32),
            pltpu.VMEM((rows * pitch, LANES), jnp.float32),
            pltpu.VMEM(code[:1] + code[2:], jnp.float32),
            pltpu.VMEM(code, jnp.bfloat16),
            pltpu.VMEM(code, jnp.bfloat16),
            pltpu.VMEM(hung[:1] + hung[2:], jnp.float32),
            pltpu.VMEM(hung, jnp.bfloat16),
            pltpu.VMEM(hung, jnp.bfloat16),
            pltpu.SemaphoreType.DMA((blocks,)),
            pltpu.SemaphoreType.DMA((5,)),
            pltpu.SemaphoreType.DMA,
            pltpu.SemaphoreType.DMA,
            pltpu.SemaphoreType.DMA(code[:4]),
            pltpu.SemaphoreType.DMA(code[:4]),
            pltpu.SemaphoreType.DMA(hung[:2]),
            pltpu.SemaphoreType.DMA(hung[:2]),
        ],
        compiler_params=pltpu.CompilerParams(
            vmem_limit_bytes=limit, collective_id=0, has_side_effects=True),
        cost_estimate=pl.CostEstimate(flops=16 * 10**9, bytes_accessed=16 << 20, transcendentals=0),
        name="channelize",
    )(*operands)
    out = out.reshape(streams, 2, tiles, spans, 8, LANES).transpose(0, 1, 2, 4, 3, 5)
    return out.reshape(streams, 2, 8 * tiles, spans * LANES)


def solution(mesh):
    in_specs = (P("stream", None, "tm"), P())
    out_specs = P("stream", None, "tm", None)
    body = functools.partial(shards, mesh.shape["tm"])
    return jax.shard_map(body, mesh=mesh, in_specs=in_specs, out_specs=out_specs, check_vma=False)
```

time: 65.3 us -> 61.9 us (0.948)
  Pallas kernels: 61.7 us -> 58 us
    pallas_call x1, Pallas kernels: 61.7 us -> 58 us  [shards(): pl.pallas_call(functools.partial(channelize, parts, streams, frames, rows...]
where the time goes in v3:
time: 61.9 us; the launch traced here: 61.4 us
  Pallas kernels  58 us (94%)
  local copies, waits for them, and re-layouts  3.4 us (5%)
    pallas_call x1, Pallas kernels, shards(): pl.pallas_call(functools.partial(channelize, parts, streams, frames, rows...  58 us
    unnamed x1, local copies, waits for them, and re-layouts  3.4 us

profile of v3, /device:TPU:0, one launch (start us, length us, event | category | flops | bytes accessed | tf_op | source)
XLA Modules:
  0.0 61.4 jit_solution(579041461513806707)
XLA Ops:
  0.0 58.0 %channelize.1 = f32[2,2,4096,128]{3,2,1,0:T(8,128)S(1)} custom-call(bf16[2,128,64,128]{3,2,1,0:T(8,128)(2,1)} %bitcast.14, f32[2,32,8,128]{3,2,1,0:T(8,128)} %bitcast.15, bf16[256,768]{1,0:T(8,128)(2,1)} %constant.10.clone.first_hbm, f32[32,128]{1,0:T(8,128)} %constant.8.clone.cos_hbm, f32[32,128]{1,0:T(8,128)} %constant.9.clone.sin_hbm, ...), custom_call_target="tpu_custom_call" | custom-call | flops 16000000000 | bytes 16777216 | tf_op jit(solution)/shard_map/channelize/pallas_call | solution.py:365
  58.0 3.4 %copy.9 = f32[2,2,2048,256]{3,2,1,0:T(8,128)} copy(f32[2,2,2048,256]{3,2,1,0:T(8,128)S(1)} %bitcast.13) | data formatting | bytes 16777216

commit v4 on v3

--- a/solution.py
+++ b/solution.py
@@ -70,9 +70,60 @@
     return high, low
 
 
+def equalize(parts, s, step, own, recv, own_over, recv_over, put):
+    me = lax.axis_index("tm")
+    blocks, each = own.shape[1], own.shape[5]
+    spans = blocks * SPAN // LANES
+    quad = WIDE // SPAN
+    group = own.shape[2] * quad // own_over.shape[1]
+    over = WIDE // group
+    lanes = lax.broadcasted_iota(jnp.int32, (each, LANES), 1)
+    left = lanes < SPAN
+
+    def fetch(k, b, j, p):
+        if k == 0:
+            return own[s, b, step, j, p]
+        return decode(recv[s, k - 1, b, step, j, p])
+
+    def hung(k, c, p):
+        at, slot = c // group, (c % group) // (LANES // over)
+        if k == 0:
+            value = own_over[s - 1, at, slot, p]
+        else:
+            value = decode(recv_over[s - 1, k - 1, at, slot, p])
+        turn = lax.rem(LANES - (c % (LANES // over)) * over, LANES)
+        return jnp.where(lanes < over, pltpu.roll(value, turn, 1), 0.0)
+
+    for j in range(WIDE // LANES):
+        whole = [[[], []] for _ in range(LANES // SPAN)]
+        for k in range(parts):
+            for p in range(2):
+                for u in range(spans):
+                    low, high = fetch(k, 2 * u, j, p), fetch(k, 2 * u + 1, j, p)
+                    whole[0][p].append(jnp.where(left, low, pltpu.roll(high, SPAN, 1)))
+                    whole[1][p].append(jnp.where(left, pltpu.roll(low, SPAN, 1), high))
+        for i in range(LANES // SPAN):
+            c = step * quad + j * (LANES // SPAN) + i
+            data = whole[i]
+            if s > 0:
+                for k in range(parts):
+                    source = lax.rem(me + parts - k, parts)
+                    for p in range(2):
+                        extra = jnp.where(source > 0, hung((k + 1) % parts, c, p), 0.0)
+                        data[p][k * spans] = data[p][k * spans] + extra
+            square = sum(a * a + b * b for a, b in zip(*data))
+            power = jnp.sum(square, axis=1, keepdims=True)
+            factor = lax.rsqrt(power * (1.0 / (parts * spans * LANES)) + 1.0)
+            for k in range(parts):
+                source = lax.rem(me + parts - k, parts) * spans
+                for p in range(2):
+                    for u in range(spans):
+                        put(p, c, source + u, data[p][k * spans + u] * factor)
+
+
 def channelize(parts, streams, frames, rows, depth, x_hbm, taps_hbm, first_hbm, cos_hbm, sin_hbm,
-               second_hbm, out_ref, xbuf, taps_raw, taps_ref, first_ref, cos_ref, sin_ref, second_ref,
-               halo, wide, grid, zr, zi, own, send, recv, own_over, send_over, recv_over,
+               second_hbm, out_ref, own, recv, own_over, recv_over, xbuf, taps_raw, taps_ref,
+               first_ref, cos_ref, sin_ref, second_ref, halo, wide, grid, zr, zi, send, send_over,
                x_sem, table_sem, halo_send, halo_recv, send_sem, recv_sem, over_send, over_recv):
     me = lax.axis_index("tm")
     each = LANES // parts
@@ -196,54 +247,16 @@
                     theirs[k - 1][j, p] = encode(out[row : row + each, lane])
 
     def finish(s, step):
-        lanes = lax.broadcasted_iota(jnp.int32, (each, LANES), 1)
         for k in range(1, parts):
             for b in range(blocks):
                 piece(s, k, b, step).wait_recv()
-
-        def fetch(k, b, j, p):
-            if k == 0:
-                return own[s, b, step, j, p]
-            return decode(recv[s, k - 1, b, step, j, p])
-
-        def hung(k, c, p):
-            at, slot = c // group, (c % group) // (LANES // over)
-            if k == 0:
-                value = own_over[s - 1, at, slot, p]
-            else:
-                value = decode(recv_over[s - 1, k - 1, at, slot, p])
-            turn = lax.rem(LANES - (c % (LANES // over)) * over, LANES)
-            return jnp.where(lanes < over, pltpu.roll(value, turn, 1), 0.0)
-
-        for j in range(WIDE // LANES):
-            whole = [[[], []] for _ in range(LANES // SPAN)]
-            for k in range(parts):
-                for p in range(2):
-                    for u in range(frames // LANES):
-                        low, high = fetch(k, 2 * u, j, p), fetch(k, 2 * u + 1, j, p)
-                        left = lanes < SPAN
-                        whole[0][p].append(jnp.where(left, low, pltpu.roll(high, SPAN, 1)))
-                        whole[1][p].append(jnp.where(left, pltpu.roll(low, SPAN, 1), high))
-            for i in range(LANES // SPAN):
-                c = step * quad + j * (LANES // SPAN) + i
-                data = whole[i]
-                if s > 0:
-                    for k in range(parts):
-                        source = lax.rem(me + parts - k, parts)
-                        for p in range(2):
-                            extra = jnp.where(source > 0, hung((k + 1) % parts, c, p), 0.0)
-                            at = k * (frames // LANES)
-                            data[p][at] = data[p][at] + extra
-                square = sum(a * a + b * b for a, b in zip(*data))
-                power = jnp.sum(square, axis=1, keepdims=True)
-                factor = lax.rsqrt(power * (1.0 / (frames * parts)) + 1.0)
-                top = (c // 8) * (8 * spans) + c % 8
-                for k in range(parts):
-                    source = lax.rem(me + parts - k, parts) * (frames // LANES)
-                    for p in range(2):
-                        for u in range(frames // LANES):
-                            row = pl.ds(top + (source + u) * 8, each, stride=rows * spans)
-                            out_ref[s, p, row, :] = data[p][k * (frames // LANES) + u] * factor
+        pitch = out_ref.shape[2] // each
+
+        def put(p, c, span, value):
+            row = pl.ds((c // 8) * (8 * spans) + span * 8 + c % 8, each, stride=pitch)
+            out_ref[s, p, row, :] = value
+
+        equalize(parts, s, step, own, recv, own_over, recv_over, put)
 
     for s in range(streams):
         for b in reversed(range(blocks)):
@@ -314,9 +327,17 @@
                 def _():
                     overhang(s, k).wait_recv()
 
-        @pl.loop(0, steps)
+        early = steps if s + 1 < streams else steps - 8 // quad
+
+        @pl.loop(0, early)
         def _(step):
             finish(s, step)
+
+        @pl.loop(early, steps)
+        def _(step):
+            for k in range(1, parts):
+                for b in range(blocks):
+                    piece(s, k, b, step).wait_recv()
 
     for s in range(streams):
 
@@ -332,6 +353,40 @@
         for s in range(1, streams):
             for k in range(1, parts):
                 overhang(s, k).wait_send()
+
+
+def deliver(parts, planes, own, recv, own_over, recv_over, out_ref, tail, plane_sem, tail_sem):
+    streams, each = own.shape[0], own.shape[5]
+    rows = out_ref.shape[3]
+    steps, quad = own.shape[2], WIDE // SPAN
+    last = streams - 1
+    spans = rows // (steps * quad)
+    ready = rows - 8 * spans
+    pitch = tail.shape[1] // each
+    copies = []
+    for s in range(streams):
+        for p in range(2):
+            pick = pl.ds(0, rows if s < last else ready)
+            copies.append(pltpu.make_async_copy(
+                planes.at[s, p, :, pick], out_ref.at[s, p, :, pick], plane_sem.at[s, p]))
+    for copy in copies:
+        copy.start()
+
+    def put(p, c, span, value):
+        tail[p, pl.ds(span * 8 + c % 8, each, stride=pitch), :] = value
+
+    @pl.loop(steps - 8 // quad, steps)
+    def _(step):
+        equalize(parts, last, step, own, recv, own_over, recv_over, put)
+
+    for p in range(2):
+        source = tail.at[p].reshape(each, pitch, LANES).at[:, pl.ds(0, 8 * spans)]
+        copies.append(pltpu.make_async_copy(
+            source, out_ref.at[last, p, :, pl.ds(ready, 8 * spans)], tail_sem.at[p]))
+    for copy in copies[-2:]:
+        copy.start()
+    for copy in copies:
+        copy.wait()
 
 
 def shards(parts, signal, taps):
@@ -362,11 +417,19 @@
     hung = (streams - 1, parts - 1, rows * over // WIDE, WIDE // LANES, 2, each, LANES)
     operands = [x, taps, first, cos, sin, second]
     operands = [pltpu.with_memory_space_constraint(a, pltpu.HBM) for a in operands]
-    out = pl.pallas_call(
+    far = rows * spans + 8
+    vmem = pl.BlockSpec(memory_space=pltpu.VMEM)
+    kept = pl.pallas_call(
         functools.partial(channelize, parts, streams, frames, rows, depth),
         in_specs=[hbm] * 6,
-        out_specs=pl.BlockSpec(memory_space=pltpu.VMEM),
-        out_shape=pltpu.VMEM((streams, 2, 8 * tiles * spans, LANES), jnp.float32),
+        out_specs=[vmem] * 5,
+        out_shape=[
+            pltpu.VMEM((streams, 2, each * far, LANES), jnp.float32),
+            pltpu.VMEM(code[:1] + code[2:], jnp.float32),
+            pltpu.VMEM(code, jnp.bfloat16),
+            pltpu.VMEM(hung[:1] + hung[2:], jnp.float32),
+            pltpu.VMEM(hung, jnp.bfloat16),
+        ],
         scratch_shapes=[
             pltpu.VMEM((frames, 2 * rows, LANES), jnp.bfloat16),
             pltpu.VMEM(taps.shape, jnp.float32),
@@ -380,11 +443,7 @@
             pltpu.VMEM((2 * GROUP * rows, 2 * LANES), jnp.float32),
             pltpu.VMEM((rows * pitch, LANES), jnp.float32),
             pltpu.VMEM((rows * pitch, LANES), jnp.float32),
-            pltpu.VMEM(code[:1] + code[2:], jnp.float32),
             pltpu.VMEM(code, jnp.bfloat16),
-            pltpu.VMEM(code, jnp.bfloat16),
-            pltpu.VMEM(hung[:1] + hung[2:], jnp.float32),
-            pltpu.VMEM(hung, jnp.bfloat16),
             pltpu.VMEM(hung, jnp.bfloat16),
             pltpu.SemaphoreType.DMA((blocks,)),
             pltpu.SemaphoreType.DMA((5,)),
@@ -400,6 +459,22 @@
         cost_estimate=pl.CostEstimate(flops=16 * 10**9, bytes_accessed=16 << 20, transcendentals=0),
         name="channelize",
     )(*operands)
+    kept = [kept[0].reshape(streams, 2, each, far, LANES), *kept[1:]]
+    kept = [pltpu.with_memory_space_constraint(a, pltpu.VMEM) for a in kept]
+    out = pl.pallas_call(
+        functools.partial(deliver, parts),
+        in_specs=[vmem] * 5,
+        out_specs=hbm,
+        out_shape=jax.ShapeDtypeStruct((streams, 2, each, rows * spans, LANES), jnp.float32),
+        scratch_shapes=[
+            pltpu.VMEM((2, each * (8 * spans + 8), LANES), jnp.float32),
+            pltpu.SemaphoreType.DMA((streams, 2)),
+            pltpu.SemaphoreType.DMA((2,)),
+        ],
+        compiler_params=pltpu.CompilerParams(vmem_limit_bytes=limit),
+        cost_estimate=pl.CostEstimate(flops=10**7, bytes_accessed=16 << 20, transcendentals=0),
+        name="deliver",
+    )(*kept)
     out = out.reshape(streams, 2, tiles, spans, 8, LANES).transpose(0, 1, 2, 4, 3, 5)
     return out.reshape(streams, 2, 8 * tiles, spans * LANES)
 

time: 61.9 us -> 60.4 us (0.976)
  local copies, waits for them, and re-layouts: 3.4 us -> 0 us
  Pallas kernels: 58 us -> 60.1 us
    unnamed x1 -> x0, local copies, waits for them, and re-layouts: 3.4 us -> none
    pallas_call x0 -> x1, Pallas kernels: none -> 3.33 us  [shards(): pl.pallas_call(functools.partial(deliver, parts), in_specs=[vmem] * 5, ou...]
    pallas_call x1, Pallas kernels: 58 us -> 56.8 us  [shards(): pl.pallas_call(functools.partial(channelize, parts, streams, frames, rows...]
where the time goes in v4:
time: 60.4 us; the launch traced here: 60.2 us
  Pallas kernels  60.1 us (100%)
    pallas_call x1, Pallas kernels, shards(): pl.pallas_call(functools.partial(channelize, parts, streams, frames, rows...  56.8 us
    pallas_call x1, Pallas kernels, shards(): pl.pallas_call(functools.partial(deliver, parts), in_specs=[vmem] * 5, ou...  3.33 us

profile of v4, /device:TPU:0, one launch (start us, length us, event | category | flops | bytes accessed | tf_op | source)
XLA Modules:
  0.0 60.2 jit_solution(14843866259228565519)
XLA Ops:
  0.0 56.8 %channelize.1 = (f32[2,2,4608,128]{3,2,1,0:T(8,128)S(1)}, f32[2,2,8,2,2,64,128]{6,5,4,3,2,1,0:T(8,128)S(1)}, bf16[2,1,2,8,2,2,64,128]{7,6,5,4,3,2,1,0:T(8,128)(2...) custom-call(bf16[2,128,64,128]{3,2,1,0:T(8,128)(2,1)} %bitcast.15, ...), custom_call_target="tpu_custom_call" | custom-call | flops 16000000000 | bytes 16777216 | tf_op jit(solution)/shard_map/channelize/pallas_call | solution.py:422
  56.8 3.3 %deliver.1 = f32[2,2,64,64,128]{4,3,2,1,0:T(8,128)} custom-call(f32[2,2,64,72,128]{4,3,2,1,0:T(8,128)S(1)} %bitcast.14, f32[2,2,8,2,2,64,128]{6,5,4,3,2,1,0:T(8,128)S(1)} %get-tuple-element.11.own, bf16[2,1,2,8,2,2,64,128]{7,6,5,4,3,2,1,0:T(8,128)(2,1)S(1)} %get-tuple-element.12.recv, f32[1,2,2,2,64,128]{5,4,3,2,1,0:T(8,128)S(1)} %get-tuple-element.13.own_over, ...), custom_call_target="tpu_custom_call" | custom-call | flops 10000000 | bytes 16777216 | tf_op jit(solution)/shard_map/deliver/pallas_call | solution.py:464

commit v5 on v4

--- a/solution.py
+++ b/solution.py
@@ -12,7 +12,8 @@
 LANES = 128
 GROUP = 4
 BATCH = 2 * GROUP
-SPAN = 64
+SPAN = 32
+CHUNK = 16
 WIDE = 2 * LANES
 POWER = 6
 SCALE = 64.0
@@ -73,52 +74,62 @@
 def equalize(parts, s, step, own, recv, own_over, recv_over, put):
     me = lax.axis_index("tm")
     blocks, each = own.shape[1], own.shape[5]
-    spans = blocks * SPAN // LANES
+    fold = LANES // SPAN
+    spans = blocks // fold
     quad = WIDE // SPAN
     group = own.shape[2] * quad // own_over.shape[1]
     over = WIDE // group
-    lanes = lax.broadcasted_iota(jnp.int32, (each, LANES), 1)
-    left = lanes < SPAN
-
-    def fetch(k, b, j, p):
-        if k == 0:
-            return own[s, b, step, j, p]
-        return decode(recv[s, k - 1, b, step, j, p])
-
-    def hung(k, c, p):
-        at, slot = c // group, (c % group) // (LANES // over)
-        if k == 0:
-            value = own_over[s - 1, at, slot, p]
-        else:
-            value = decode(recv_over[s - 1, k - 1, at, slot, p])
-        turn = lax.rem(LANES - (c % (LANES // over)) * over, LANES)
-        return jnp.where(lanes < over, pltpu.roll(value, turn, 1), 0.0)
-
-    for j in range(WIDE // LANES):
-        whole = [[[], []] for _ in range(LANES // SPAN)]
-        for k in range(parts):
-            for p in range(2):
-                for u in range(spans):
-                    low, high = fetch(k, 2 * u, j, p), fetch(k, 2 * u + 1, j, p)
-                    whole[0][p].append(jnp.where(left, low, pltpu.roll(high, SPAN, 1)))
-                    whole[1][p].append(jnp.where(left, pltpu.roll(low, SPAN, 1), high))
-        for i in range(LANES // SPAN):
-            c = step * quad + j * (LANES // SPAN) + i
-            data = whole[i]
-            if s > 0:
+    lanes = lax.broadcasted_iota(jnp.int32, (CHUNK, LANES), 1)
+    segment = lanes // SPAN
+    sources = [lax.rem(me + parts - k, parts) for k in range(parts)]
+
+    def move(value, shift):
+        return pltpu.roll(value, shift % LANES, 1) if shift % LANES else value
+
+    for r in range(0, each, CHUNK):
+        sub = slice(r, r + CHUNK)
+
+        def fetch(k, b, j, p):
+            if k == 0:
+                return own[s, b, step, j, p, sub]
+            return decode(recv[s, k - 1, b, step, j, p, sub])
+
+        def hung(k, p):
+            at, slot = step * quad // group, step * quad % group // (LANES // over)
+            if k == 0:
+                return own_over[s - 1, at, slot, p, sub]
+            return decode(recv_over[s - 1, k - 1, at, slot, p, sub])
+
+        if s > 0:
+            extras = [[jnp.where(sources[k] > 0, hung((k + 1) % parts, p), 0.0)
+                       for p in range(2)] for k in range(parts)]
+
+        for j in range(WIDE // LANES):
+            tiles = [[[fetch(k, b, j, p) for b in range(blocks)] for p in range(2)]
+                     for k in range(parts)]
+            for i in range(fold):
+                n = j * fold + i
+                data = [[], []]
                 for k in range(parts):
-                    source = lax.rem(me + parts - k, parts)
                     for p in range(2):
-                        extra = jnp.where(source > 0, hung((k + 1) % parts, c, p), 0.0)
-                        data[p][k * spans] = data[p][k * spans] + extra
-            square = sum(a * a + b * b for a, b in zip(*data))
-            power = jnp.sum(square, axis=1, keepdims=True)
-            factor = lax.rsqrt(power * (1.0 / (parts * spans * LANES)) + 1.0)
-            for k in range(parts):
-                source = lax.rem(me + parts - k, parts) * spans
-                for p in range(2):
-                    for u in range(spans):
-                        put(p, c, source + u, data[p][k * spans + u] * factor)
+                        for u in range(spans):
+                            value = tiles[k][p][u * fold]
+                            for q in range(1, fold):
+                                here = segment == (i + q) % fold
+                                value = jnp.where(here, tiles[k][p][u * fold + q], value)
+                            if s > 0 and u == 0:
+                                extra = move(extras[k][p], -j * over)
+                                inside = (segment == i) & (lanes % SPAN < over)
+                                value = value + jnp.where(inside, extra, 0.0)
+                            data[p].append(move(value, -i * SPAN))
+                square = sum(a * a + b * b for a, b in zip(*data))
+                power = jnp.sum(square, axis=1, keepdims=True)
+                factor = lax.rsqrt(power * (1.0 / (parts * spans * LANES)) + 1.0)
+                for k in range(parts):
+                    for p in range(2):
+                        for u in range(spans):
+                            put(p, step * quad + n, n, sources[k] * spans + u, r,
+                                data[p][k * spans + u] * factor)
 
 
 def channelize(parts, streams, frames, rows, depth, x_hbm, taps_hbm, first_hbm, cos_hbm, sin_hbm,
@@ -131,6 +142,7 @@
     over = -(-past // BATCH) * BATCH
     blocks = frames // SPAN
     quad = WIDE // SPAN
+    fold = LANES // SPAN
     steps = rows // quad
     group = WIDE // over
     spans = frames * parts // LANES
@@ -173,16 +185,15 @@
     ]
     for table in tables:
         table.start()
-    for b in reversed(range(blocks - 1)):
-        load(0, b).start()
     pl.semaphore_wait(barrier, parts - 1)
 
     @pl.when(me < parts - 1)
     def _():
         edge().start()
 
-    for table in tables:
-        table.wait()
+    for b in reversed(range(blocks - 1)):
+        load(0, b).start()
+    tables[0].wait()
 
     @pl.loop(0, rows)
     def _(n):
@@ -190,8 +201,6 @@
             for p in range(2):
                 row = pl.ds(g * 8 * reach + 2 * n + p, 8, stride=reach)
                 taps_ref[row, :] = taps_raw[g, n]
-
-    wide[past + frames :] = jnp.zeros((over, 2 * rows, LANES), jnp.float32)
 
     def widen(s, b):
         load(s, b).wait()
@@ -227,10 +236,10 @@
             zr[pick, :] = real * cos + imag * sin
             zi[pick, :] = imag * cos - real * sin
 
-    def second_stage(step, count, length, pitch):
+    def second_stage(step, order, length, pitch):
         pieces = []
-        for i in range(count):
-            pick = pl.ds(pl.multiple_of((step * count + i) * pitch, 8), length)
+        for i in order:
+            pick = pl.ds(pl.multiple_of((step * len(order) + i) * pitch, 8), length)
             pieces.append(jnp.concatenate([zr[pick, :], zi[pick, :]], axis=1))
         high, low = halves(jnp.concatenate(pieces, axis=0))
         top = pl.ds(pl.multiple_of(me * 2 * each, 2 * each), 2 * LANES)
@@ -252,9 +261,9 @@
                 piece(s, k, b, step).wait_recv()
         pitch = out_ref.shape[2] // each
 
-        def put(p, c, span, value):
-            row = pl.ds((c // 8) * (8 * spans) + span * 8 + c % 8, each, stride=pitch)
-            out_ref[s, p, row, :] = value
+        def put(p, c, n, span, r, value):
+            top = (c // 8) * (8 * spans) + span * 8 + n % 8
+            out_ref[s, p, pl.ds(top + r * pitch, CHUNK, stride=pitch), :] = value
 
         equalize(parts, s, step, own, recv, own_over, recv_over, put)
 
@@ -288,14 +297,22 @@
                 if s == 1:
                     wide[:past] = jnp.zeros((past, 2 * rows, LANES), jnp.float32)
 
+            if s == 0 and b == blocks - 1:
+                for table in tables[1:4]:
+                    table.wait()
+
             @pl.loop(0, SPAN // BATCH)
             def _(step):
                 base = pl.multiple_of(step * BATCH, BATCH)
                 first_stage(b * SPAN + base, base, SPAN + 8)
 
+            if s == 0 and b == blocks - 1:
+                tables[4].wait()
+
             @pl.loop(0, steps)
             def _(step):
-                out = second_stage(step, quad, SPAN, SPAN + 8)
+                order = [j + (i - b) % fold for j in range(0, quad, fold) for i in range(fold)]
+                out = second_stage(step, order, SPAN, SPAN + 8)
                 keep(out, own.at[s, b, step], [send.at[s, k, b, step] for k in range(parts - 1)])
 
                 @pl.when(step > 0)
@@ -306,6 +323,9 @@
             for k in range(1, parts):
                 piece(s, k, b, steps - 1).start()
 
+            if s == 1 and b == blocks - 1:
+                wide[past + frames :] = jnp.zeros((over, 2 * rows, LANES), jnp.float32)
+
             if s > 0 and b == blocks - 1:
 
                 @pl.loop(0, over // BATCH)
@@ -315,7 +335,9 @@
 
                 @pl.loop(0, rows // group)
                 def _(step):
-                    out = second_stage(step, group, over, over + 8)
+                    order = [j + i % 2 * fold + i // 2
+                             for j in range(0, group, 2 * fold) for i in range(2 * fold)]
+                    out = second_stage(step, order, over, over + 8)
                     keep(out, own_over.at[s - 1, step],
                          [send_over.at[s - 1, k, step] for k in range(parts - 1)])
 
@@ -372,8 +394,8 @@
     for copy in copies:
         copy.start()
 
-    def put(p, c, span, value):
-        tail[p, pl.ds(span * 8 + c % 8, each, stride=pitch), :] = value
+    def put(p, c, n, span, r, value):
+        tail[p, pl.ds(span * 8 + n % 8 + r * pitch, CHUNK, stride=pitch), :] = value
 
     @pl.loop(steps - 8 // quad, steps)
     def _(step):

time: 60.4 us -> 65.6 us (1.086)
  the two profiles are of different devices: /device:TPU:0 before, /device:TPU:2 now
where the time goes in v5:
time: 65.6 us; the launch traced here: 65.4 us
  Pallas kernels  65.4 us (100%)
    pallas_call x1, Pallas kernels, shards(): pl.pallas_call(functools.partial(channelize, parts, streams, frames, rows...  60.1 us
    pallas_call x1, Pallas kernels, shards(): pl.pallas_call(functools.partial(deliver, parts), in_specs=[vmem] * 5, ou...  5.31 us

profile of v5, /device:TPU:2, one launch (start us, length us, event | category | flops | bytes accessed | tf_op | source)
XLA Modules:
  0.0 65.4 jit_solution(524805096847076030)
XLA Ops:
  0.0 60.1 %channelize.1 = (f32[2,2,4608,128]{3,2,1,0:T(8,128)S(1)}, f32[2,4,4,2,2,64,128]{6,5,4,3,2,1,0:T(8,128)S(1)}, bf16[2,1,4,4,2,2,64,128]{7,6,5,4,3,2,1,0:T(8,128)(2...) custom-call(bf16[2,128,64,128]{3,2,1,0:T(8,128)(2,1)} %bitcast.15, ...), custom_call_target="tpu_custom_call" | custom-call | flops 16000000000 | bytes 16777216 | tf_op jit(solution)/shard_map/channelize/pallas_call | solution.py:444
  60.1 5.3 %deliver.1 = f32[2,2,64,64,128]{4,3,2,1,0:T(8,128)} custom-call(f32[2,2,64,72,128]{4,3,2,1,0:T(8,128)S(1)} %bitcast.14, f32[2,4,4,2,2,64,128]{6,5,4,3,2,1,0:T(8,128)S(1)} %get-tuple-element.11.own, bf16[2,1,4,4,2,2,64,128]{7,6,5,4,3,2,1,0:T(8,128)(2,1)S(1)} %get-tuple-element.12.recv, f32[1,2,2,2,64,128]{5,4,3,2,1,0:T(8,128)S(1)} %get-tuple-element.13.own_over, ...), custom_call_target="tpu_custom_call" | custom-call | flops 10000000 | bytes 16777216 | tf_op jit(solution)/shard_map/deliver/pallas_call | solution.py:486

commit v6 on v5

--- a/solution.py
+++ b/solution.py
@@ -81,6 +81,7 @@
     over = WIDE // group
     lanes = lax.broadcasted_iota(jnp.int32, (CHUNK, LANES), 1)
     segment = lanes // SPAN
+    ones = jnp.ones((2 * LANES, LANES), jnp.bfloat16)
     sources = [lax.rem(me + parts - k, parts) for k in range(parts)]
 
     def move(value, shift):
@@ -107,8 +108,8 @@
         for j in range(WIDE // LANES):
             tiles = [[[fetch(k, b, j, p) for b in range(blocks)] for p in range(2)]
                      for k in range(parts)]
+            merged, squares = [], []
             for i in range(fold):
-                n = j * fold + i
                 data = [[], []]
                 for k in range(parts):
                     for p in range(2):
@@ -121,15 +122,21 @@
                                 extra = move(extras[k][p], -j * over)
                                 inside = (segment == i) & (lanes % SPAN < over)
                                 value = value + jnp.where(inside, extra, 0.0)
-                            data[p].append(move(value, -i * SPAN))
-                square = sum(a * a + b * b for a, b in zip(*data))
-                power = jnp.sum(square, axis=1, keepdims=True)
-                factor = lax.rsqrt(power * (1.0 / (parts * spans * LANES)) + 1.0)
+                            data[p].append(value)
+                merged.append(data)
+                squares.append(sum(a * a + b * b for a, b in zip(*data)))
+            parted = jnp.concatenate(halves(jnp.concatenate(squares, axis=0)), axis=1)
+            power = jnp.dot(parted, ones, preferred_element_type=jnp.float32)
+            factor = lax.rsqrt(power * (1.0 / (parts * spans * LANES)) + 1.0)
+            for i in range(fold):
+                n = j * fold + i
+                scale = factor[i * CHUNK : (i + 1) * CHUNK]
                 for k in range(parts):
                     for p in range(2):
                         for u in range(spans):
+                            value = merged[i][p][k * spans + u] * scale
                             put(p, step * quad + n, n, sources[k] * spans + u, r,
-                                data[p][k * spans + u] * factor)
+                                move(value, -i * SPAN))
 
 
 def channelize(parts, streams, frames, rows, depth, x_hbm, taps_hbm, first_hbm, cos_hbm, sin_hbm,

time: 65.6 us -> 60.3 us (0.919)
  the two profiles are of different devices: /device:TPU:2 before, /device:TPU:0 now
where the time goes in v6:
time: 60.3 us; the launch traced here: 60.2 us
  Pallas kernels  60.2 us (100%)
    pallas_call x1, Pallas kernels, shards(): pl.pallas_call(functools.partial(channelize, parts, streams, frames, rows...  56.8 us
    pallas_call x1, Pallas kernels, shards(): pl.pallas_call(functools.partial(deliver, parts), in_specs=[vmem] * 5, ou...  3.34 us

profile of v6, /device:TPU:0, one launch (start us, length us, event | category | flops | bytes accessed | tf_op | source)
XLA Modules:
  0.0 60.2 jit_solution(844179392550826225)
XLA Ops:
  0.0 56.8 %channelize.1 = (f32[2,2,4608,128]{3,2,1,0:T(8,128)S(1)}, f32[2,4,4,2,2,64,128]{6,5,4,3,2,1,0:T(8,128)S(1)}, bf16[2,1,4,4,2,2,64,128]{7,6,5,4,3,2,1,0:T(8,128)(2...) custom-call(bf16[2,128,64,128]{3,2,1,0:T(8,128)(2,1)} %bitcast.15, ...), custom_call_target="tpu_custom_call" | custom-call | flops 16000000000 | bytes 16777216 | tf_op jit(solution)/shard_map/channelize/pallas_call | solution.py:451
  56.8 3.3 %deliver.1 = f32[2,2,64,64,128]{4,3,2,1,0:T(8,128)} custom-call(f32[2,2,64,72,128]{4,3,2,1,0:T(8,128)S(1)} %bitcast.14, f32[2,4,4,2,2,64,128]{6,5,4,3,2,1,0:T(8,128)S(1)} %get-tuple-element.11.own, bf16[2,1,4,4,2,2,64,128]{7,6,5,4,3,2,1,0:T(8,128)(2,1)S(1)} %get-tuple-element.12.recv, f32[1,2,2,2,64,128]{5,4,3,2,1,0:T(8,128)S(1)} %get-tuple-element.13.own_over, ...), custom_call_target="tpu_custom_call" | custom-call | flops 10000000 | bytes 16777216 | tf_op jit(solution)/shard_map/deliver/pallas_call | solution.py:493

commit v7 on v6

--- a/solution.py
+++ b/solution.py
@@ -78,7 +78,7 @@
     spans = blocks // fold
     quad = WIDE // SPAN
     group = own.shape[2] * quad // own_over.shape[1]
-    over = WIDE // group
+    over = BATCH if s == 0 else WIDE // group
     lanes = lax.broadcasted_iota(jnp.int32, (CHUNK, LANES), 1)
     segment = lanes // SPAN
     ones = jnp.ones((2 * LANES, LANES), jnp.bfloat16)
@@ -96,14 +96,13 @@
             return decode(recv[s, k - 1, b, step, j, p, sub])
 
         def hung(k, p):
-            at, slot = step * quad // group, step * quad % group // (LANES // over)
+            at, slot = (0, step // 2) if s == 0 else (step // 2, step % 2)
             if k == 0:
-                return own_over[s - 1, at, slot, p, sub]
-            return decode(recv_over[s - 1, k - 1, at, slot, p, sub])
-
-        if s > 0:
-            extras = [[jnp.where(sources[k] > 0, hung((k + 1) % parts, p), 0.0)
-                       for p in range(2)] for k in range(parts)]
+                return own_over[s, at, slot, p, sub]
+            return decode(recv_over[s, k - 1, at, slot, p, sub])
+
+        extras = [[jnp.where(sources[k] > 0, hung((k + 1) % parts, p), 0.0)
+                   for p in range(2)] for k in range(parts)]
 
         for j in range(WIDE // LANES):
             tiles = [[[fetch(k, b, j, p) for b in range(blocks)] for p in range(2)]
@@ -118,8 +117,12 @@
                             for q in range(1, fold):
                                 here = segment == (i + q) % fold
                                 value = jnp.where(here, tiles[k][p][u * fold + q], value)
-                            if s > 0 and u == 0:
-                                extra = move(extras[k][p], -j * over)
+                            if u == 0:
+                                if s == 0:
+                                    shift = LANES - (step % 2 * 2 + j) * over
+                                    extra = pltpu.roll(extras[k][p], lax.rem(shift, LANES), 1)
+                                else:
+                                    extra = move(extras[k][p], -j * over)
                                 inside = (segment == i) & (lanes % SPAN < over)
                                 value = value + jnp.where(inside, extra, 0.0)
                             data[p].append(value)
@@ -147,11 +150,11 @@
     each = LANES // parts
     past = depth - 1
     over = -(-past // BATCH) * BATCH
+    near = past - BATCH
     blocks = frames // SPAN
     quad = WIDE // SPAN
     fold = LANES // SPAN
     steps = rows // quad
-    group = WIDE // over
     spans = frames * parts // LANES
     reach = taps_ref.shape[0] // depth
     bounds = [max(b * SPAN - over, 0) for b in range(blocks)] + [frames]
@@ -167,7 +170,7 @@
 
     def edge():
         return pltpu.make_async_remote_copy(
-            src_ref=x_hbm.at[0, pl.ds(frames - past, past)], dst_ref=halo,
+            src_ref=x_hbm.at[0, pl.ds(frames - near, near)], dst_ref=halo,
             send_sem=halo_send, recv_sem=halo_recv,
             device_id={"tm": lax.rem(me + 1, parts)}, device_id_type=pl.DeviceIdType.MESH)
 
@@ -178,9 +181,11 @@
             device_id={"tm": lax.rem(me + k, parts)}, device_id_type=pl.DeviceIdType.MESH)
 
     def overhang(s, k):
+        units = rows * (BATCH if s == 0 else over) // WIDE
         return pltpu.make_async_remote_copy(
-            src_ref=send_over.at[s - 1, k - 1], dst_ref=recv_over.at[s - 1, k - 1],
-            send_sem=over_send.at[s - 1, k - 1], recv_sem=over_recv.at[s - 1, k - 1],
+            src_ref=send_over.at[s, k - 1, pl.ds(0, units)],
+            dst_ref=recv_over.at[s, k - 1, pl.ds(0, units)],
+            send_sem=over_send.at[s, k - 1], recv_sem=over_recv.at[s, k - 1],
             device_id={"tm": lax.rem(me + k, parts)}, device_id_type=pl.DeviceIdType.MESH)
 
     load(0, blocks - 1).start()
@@ -277,7 +282,7 @@
     for s in range(streams):
         for b in reversed(range(blocks)):
             widen(s, b)
-            if s > 0 and b == blocks - 2:
+            if b == blocks - 2:
 
                 @pl.when(me < parts - 1)
                 def _():
@@ -293,13 +298,15 @@
                     @pl.when(me > 0)
                     def _():
                         edge().wait_recv()
-                        wide[:past] = halo[...].astype(jnp.float32)
+                        wide[BATCH:past] = halo[...].astype(jnp.float32)
 
                 if s == 0:
 
                     @pl.when(me == 0)
                     def _():
-                        wide[:past] = jnp.zeros((past, 2 * rows, LANES), jnp.float32)
+                        wide[BATCH:past] = jnp.zeros((near, 2 * rows, LANES), jnp.float32)
+
+                    wide[:BATCH] = jnp.zeros((BATCH, 2 * rows, LANES), jnp.float32)
 
                 if s == 1:
                     wide[:past] = jnp.zeros((past, 2 * rows, LANES), jnp.float32)
@@ -330,31 +337,38 @@
             for k in range(1, parts):
                 piece(s, k, b, steps - 1).start()
 
-            if s == 1 and b == blocks - 1:
-                wide[past + frames :] = jnp.zeros((over, 2 * rows, LANES), jnp.float32)
-
-            if s > 0 and b == blocks - 1:
-
-                @pl.loop(0, over // BATCH)
+            if b == blocks - 1:
+                if s == 0:
+                    start, extent = past + frames, BATCH
+                    old = pl.ds(frames - past, BATCH)
+                    wide[start : start + BATCH] = xbuf[old].astype(jnp.float32)
+                    wide[start + BATCH :] = jnp.zeros((past, 2 * rows, LANES), jnp.float32)
+                    place = [(2 * t + m // 2) * quad + m % 2 * fold + i
+                             for t in range(2) for i in range(fold) for m in range(fold)]
+                else:
+                    start, extent = frames, over
+                    place = [j + i % 2 * fold + i // 2
+                             for j in range(0, WIDE // over, 2 * fold) for i in range(2 * fold)]
+                if s == 1:
+                    wide[past + frames :] = jnp.zeros((past + BATCH, 2 * rows, LANES), jnp.float32)
+
+                @pl.loop(0, extent // BATCH)
                 def _(step):
                     base = pl.multiple_of(step * BATCH, BATCH)
-                    first_stage(frames + base, base, over + 8)
-
-                @pl.loop(0, rows // group)
+                    first_stage(start + base, base, extent + 8)
+
+                @pl.loop(0, rows * extent // WIDE)
                 def _(step):
-                    order = [j + i % 2 * fold + i // 2
-                             for j in range(0, group, 2 * fold) for i in range(2 * fold)]
-                    out = second_stage(step, order, over, over + 8)
-                    keep(out, own_over.at[s - 1, step],
-                         [send_over.at[s - 1, k, step] for k in range(parts - 1)])
+                    out = second_stage(step, place, extent, extent + 8)
+                    keep(out, own_over.at[s, step],
+                         [send_over.at[s, k, step] for k in range(parts - 1)])
 
     for s in range(streams):
-        if s > 0:
-            for k in range(1, parts):
-
-                @pl.when(lax.rem(me + parts - k, parts) < parts - 1)
-                def _():
-                    overhang(s, k).wait_recv()
+        for k in range(1, parts):
+
+            @pl.when(lax.rem(me + parts - k, parts) < parts - 1)
+            def _():
+                overhang(s, k).wait_recv()
 
         early = steps if s + 1 < streams else steps - 8 // quad
 
@@ -379,7 +393,7 @@
     @pl.when(me < parts - 1)
     def _():
         edge().wait_send()
-        for s in range(1, streams):
+        for s in range(streams):
             for k in range(1, parts):
                 overhang(s, k).wait_send()
 
@@ -443,7 +457,7 @@
     limit = (8 << 20) + 2 * width + 4 * width + 4 * width * 9 // 8 + 8 * width * streams * (parts + 1) // parts
     hbm = pl.BlockSpec(memory_space=pltpu.HBM)
     code = (streams, parts - 1, blocks, steps, WIDE // LANES, 2, each, LANES)
-    hung = (streams - 1, parts - 1, rows * over // WIDE, WIDE // LANES, 2, each, LANES)
+    hung = (streams, parts - 1, rows * over // WIDE, WIDE // LANES, 2, each, LANES)
     operands = [x, taps, first, cos, sin, second]
     operands = [pltpu.with_memory_space_constraint(a, pltpu.HBM) for a in operands]
     far = rows * spans + 8
@@ -467,8 +481,8 @@
             pltpu.VMEM(cos.shape, jnp.float32),
             pltpu.VMEM(sin.shape, jnp.float32),
             pltpu.VMEM(second.shape, jnp.bfloat16),
-            pltpu.VMEM((depth - 1, 2 * rows, LANES), jnp.bfloat16),
-            pltpu.VMEM((depth - 1 + frames + over, 2 * rows, LANES), jnp.float32),
+            pltpu.VMEM((depth - 1 - BATCH, 2 * rows, LANES), jnp.bfloat16),
+            pltpu.VMEM((2 * (depth - 1) + frames + BATCH, 2 * rows, LANES), jnp.float32),
             pltpu.VMEM((2 * GROUP * rows, 2 * LANES), jnp.float32),
             pltpu.VMEM((rows * pitch, LANES), jnp.float32),
             pltpu.VMEM((rows * pitch, LANES), jnp.float32),

time: 60.3 us -> 59.4 us (0.985)
  Pallas kernels: 60.2 us -> 59.3 us
    pallas_call x1, Pallas kernels: 56.8 us -> 55.9 us  [shards(): pl.pallas_call(functools.partial(channelize, parts, streams, frames, rows...]
where the time goes in v7:
time: 59.4 us; the launch traced here: 59.3 us
  Pallas kernels  59.3 us (100%)
    pallas_call x1, Pallas kernels, shards(): pl.pallas_call(functools.partial(channelize, parts, streams, frames, rows...  55.9 us
    pallas_call x1, Pallas kernels, shards(): pl.pallas_call(functools.partial(deliver, parts), in_specs=[vmem] * 5, ou...  3.34 us

profile of v7, /device:TPU:0, one launch (start us, length us, event | category | flops | bytes accessed | tf_op | source)
XLA Modules:
  0.0 59.3 jit_solution(8382204529026996742)
XLA Ops:
  0.0 55.9 %channelize.1 = (f32[2,2,4608,128]{3,2,1,0:T(8,128)S(1)}, f32[2,4,4,2,2,64,128]{6,5,4,3,2,1,0:T(8,128)S(1)}, bf16[2,1,4,4,2,2,64,128]{7,6,5,4,3,2,1,0:T(8,128)(2...) custom-call(bf16[2,128,64,128]{3,2,1,0:T(8,128)(2,1)} %bitcast.15, ...), custom_call_target="tpu_custom_call" | custom-call | flops 16000000000 | bytes 16777216 | tf_op jit(solution)/shard_map/channelize/pallas_call | solution.py:465
  55.9 3.3 %deliver.1 = f32[2,2,64,64,128]{4,3,2,1,0:T(8,128)} custom-call(f32[2,2,64,72,128]{4,3,2,1,0:T(8,128)S(1)} %bitcast.14, f32[2,4,4,2,2,64,128]{6,5,4,3,2,1,0:T(8,128)S(1)} %get-tuple-element.11.own, bf16[2,1,4,4,2,2,64,128]{7,6,5,4,3,2,1,0:T(8,128)(2,1)S(1)} %get-tuple-element.12.recv, f32[2,2,2,2,64,128]{5,4,3,2,1,0:T(8,128)S(1)} %get-tuple-element.13.own_over, ...), custom_call_target="tpu_custom_call" | custom-call | flops 10000000 | bytes 16777216 | tf_op jit(solution)/shard_map/deliver/pallas_call | solution.py:507

commit v8 on v7

--- a/solution.py
+++ b/solution.py
@@ -197,17 +197,11 @@
     ]
     for table in tables:
         table.start()
-    pl.semaphore_wait(barrier, parts - 1)
-
-    @pl.when(me < parts - 1)
-    def _():
-        edge().start()
-
     for b in reversed(range(blocks - 1)):
         load(0, b).start()
     tables[0].wait()
 
-    @pl.loop(0, rows)
+    @pl.loop(0, rows, unroll=8)
     def _(n):
         for g in range(depth // 8):
             for p in range(2):
@@ -222,7 +216,14 @@
             base = pl.multiple_of(step * BATCH, BATCH)
             wide[pl.ds(base + past, BATCH)] = xbuf[pl.ds(base, BATCH)].astype(jnp.float32)
 
-    def first_stage(frame, slot, pitch):
+    widen(0, blocks - 1)
+    pl.semaphore_wait(barrier, parts - 1)
+
+    @pl.when(me < parts - 1)
+    def _():
+        edge().start()
+
+    def sift(frame, n):
         for block in range(2 * rows // 8):
             sub = slice(block * 8, block * 8 + 8)
             data = [wide[frame + i, sub, :] for i in range(BATCH + past)]
@@ -234,8 +235,10 @@
                     total = total + taps[k] * data[t + past - k]
                 row = (t % GROUP) * 2 * rows + block * 8
                 lane = (t // GROUP) * LANES
-                grid[row : row + 8, lane : lane + LANES] = total
-        high, low = halves(grid[...])
+                grid[n, row : row + 8, lane : lane + LANES] = total
+
+    def turn(slot, pitch, n):
+        high, low = halves(grid[n])
         out = jnp.dot(first_ref[...], jnp.concatenate([high, high, low], axis=0),
                       preferred_element_type=jnp.float32)
         cos, sin = cos_ref[...], sin_ref[...]
@@ -248,6 +251,15 @@
             zr[pick, :] = real * cos + imag * sin
             zi[pick, :] = imag * cos - real * sin
 
+    def first_stage(frame, pitch, count):
+        @pl.loop(0, count)
+        def _(n):
+            sift(frame + pl.multiple_of(n * BATCH, BATCH), n)
+
+        @pl.loop(0, count, unroll=min(count, 4))
+        def _(n):
+            turn(pl.multiple_of(n * BATCH, BATCH), pitch, n)
+
     def second_stage(step, order, length, pitch):
         pieces = []
         for i in order:
@@ -281,7 +293,8 @@
 
     for s in range(streams):
         for b in reversed(range(blocks)):
-            widen(s, b)
+            if s > 0 or b < blocks - 1:
+                widen(s, b)
             if b == blocks - 2:
 
                 @pl.when(me < parts - 1)
@@ -315,10 +328,7 @@
                 for table in tables[1:4]:
                     table.wait()
 
-            @pl.loop(0, SPAN // BATCH)
-            def _(step):
-                base = pl.multiple_of(step * BATCH, BATCH)
-                first_stage(b * SPAN + base, base, SPAN + 8)
+            first_stage(b * SPAN, SPAN + 8, SPAN // BATCH)
 
             if s == 0 and b == blocks - 1:
                 tables[4].wait()
@@ -352,10 +362,7 @@
                 if s == 1:
                     wide[past + frames :] = jnp.zeros((past + BATCH, 2 * rows, LANES), jnp.float32)
 
-                @pl.loop(0, extent // BATCH)
-                def _(step):
-                    base = pl.multiple_of(step * BATCH, BATCH)
-                    first_stage(start + base, base, extent + 8)
+                first_stage(start, extent + 8, extent // BATCH)
 
                 @pl.loop(0, rows * extent // WIDE)
                 def _(step):
@@ -483,7 +490,7 @@
             pltpu.VMEM(second.shape, jnp.bfloat16),
             pltpu.VMEM((depth - 1 - BATCH, 2 * rows, LANES), jnp.bfloat16),
             pltpu.VMEM((2 * (depth - 1) + frames + BATCH, 2 * rows, LANES), jnp.float32),
-            pltpu.VMEM((2 * GROUP * rows, 2 * LANES), jnp.float32),
+            pltpu.VMEM((SPAN // BATCH, 2 * GROUP * rows, 2 * LANES), jnp.float32),
             pltpu.VMEM((rows * pitch, LANES), jnp.float32),
             pltpu.VMEM((rows * pitch, LANES), jnp.float32),
             pltpu.VMEM(code, jnp.bfloat16),

time: 59.4 us -> 59.1 us (level)
  no operation moved by 1% of the time
where the time goes in v8:
time: 59.1 us; the launch traced here: 59 us
  Pallas kernels  58.8 us (99%)
    pallas_call x1, Pallas kernels, shards(): pl.pallas_call(functools.partial(channelize, parts, streams, frames, rows...  55.5 us
    pallas_call x1, Pallas kernels, shards(): pl.pallas_call(functools.partial(deliver, parts), in_specs=[vmem] * 5, ou...  3.34 us

profile of v8, /device:TPU:0, one launch (start us, length us, event | category | flops | bytes accessed | tf_op | source)
XLA Modules:
  0.0 59.0 jit_solution(9489738765496704045)
XLA Ops:
  0.0 55.5 %channelize.1 = (f32[2,2,4608,128]{3,2,1,0:T(8,128)S(1)}, f32[2,4,4,2,2,64,128]{6,5,4,3,2,1,0:T(8,128)S(1)}, bf16[2,1,4,4,2,2,64,128]{7,6,5,4,3,2,1,0:T(8,128)(2...) custom-call(bf16[2,128,64,128]{3,2,1,0:T(8,128)(2,1)} %bitcast.15, ...), custom_call_target="tpu_custom_call" | custom-call | flops 16000000000 | bytes 16777216 | tf_op jit(solution)/shard_map/channelize/pallas_call | solution.py:472
  55.5 3.3 %deliver.1 = f32[2,2,64,64,128]{4,3,2,1,0:T(8,128)} custom-call(f32[2,2,64,72,128]{4,3,2,1,0:T(8,128)S(1)} %bitcast.14, f32[2,4,4,2,2,64,128]{6,5,4,3,2,1,0:T(8,128)S(1)} %get-tuple-element.11.own, bf16[2,1,4,4,2,2,64,128]{7,6,5,4,3,2,1,0:T(8,128)(2,1)S(1)} %get-tuple-element.12.recv, f32[2,2,2,2,64,128]{5,4,3,2,1,0:T(8,128)S(1)} %get-tuple-element.13.own_over, ...), custom_call_target="tpu_custom_call" | custom-call | flops 10000000 | bytes 16777216 | tf_op jit(solution)/shard_map/deliver/pallas_call | solution.py:514
